TPU v7x, 32 devices: a whole 2x2x4 slice. The times are simulated.
32 devices in a mesh: row: 4 (over y, core), col: 8 (over z, x).
Axes of the slice: x: 2, y: 2, z: 4, core: 2. Of those that a mesh axis runs over, the one named last changes fastest.
Arguments:
- factors: bfloat16 [32, 2, 512, 512], P(('row', 'col')), as said below
- target: int32 [64, 1], P(('row', 'col')), may hold values from 0 to 31; in each aligned block of 64 rows (0 to 63, 64 to 127, ...) at most 3 rows name the same one
Outputs:
- roots: float32 [32, 3, 512, 512], P(('row', 'col'))
Inputs may be any that keep to these rules, and one draw needn't show every extreme that they name: `factors`: every block is symmetric and positive definite. `target`: every device receives between 1 and 3 blocks; some device receives exactly 3.
All inputs are finite; a program needn't handle non-finite values.
Results may differ from a plain program's by a relative error of at most 0.0003.
Values may be sent and summed in bfloat16 or wider, within the bound.
No kernel may reach another device: no remote copies, remote signals or barrier semaphores. Data moves between devices by JAX's collectives and lax.ppermute only.
A program may use at most 128 MiB of HBM per device.

v0:
```python
import jax
import jax.numpy as jnp
from jax import lax
from jax.sharding import PartitionSpec as P

ITERS = 3
CAP = 3


HIGH = lax.Precision.HIGHEST


def entering(part, axis, combine, identity):
    place = lax.axis_index(axis)
    gathered = lax.all_gather(part, axis)
    state = jnp.zeros_like(part) + jnp.asarray(identity, part.dtype)

    def one(turn, state):
        return combine(state, lax.dynamic_index_in_dim(gathered, turn, 0, False))

    return lax.fori_loop(0, place, one, state)


def as_sent(value):
    return jax.tree.map(lambda a: a.astype(jnp.bfloat16) if a.dtype == jnp.float32 else a, value)


def add_counts(earlier, later):
    return earlier + later


def bucket(blocks, labels, group_keys, places, groups, room):
    item_total = blocks.shape[0]
    block_width = blocks.shape[1]
    wanted = jnp.where(labels[:, 0] > 0, group_keys * room + places, -1)
    chooser = jnp.arange(groups * room, dtype=jnp.int32)[:, None] == wanted[None, :]
    placed = jnp.dot(
        chooser.astype(jnp.bfloat16),
        blocks.reshape(item_total, block_width * block_width),
        preferred_element_type=jnp.float32,
    )
    placed = placed.astype(jnp.bfloat16).reshape(groups * room, block_width, block_width)
    placed_labels = jnp.dot(chooser.astype(jnp.int32), labels)
    return (placed, placed_labels)


def shards(factors, target):
    row_count = lax.axis_size("row")
    col_count = lax.axis_size("col")
    device_count = row_count * col_count
    hold_count = factors.shape[1]
    block_width = factors.shape[2]
    my_row = lax.axis_index("row")
    targets = target[:, 0]
    peer_ids = jnp.arange(device_count, dtype=jnp.int32)
    matches = (targets[:, None] == peer_ids[None, :]).astype(jnp.int32)
    offsets_in = entering(
        jnp.sum(matches, axis=0), ("row", "col"), add_counts, jnp.zeros((device_count,), jnp.int32)
    )
    earlier = jnp.cumsum(matches, axis=0) - matches
    slot_index = jnp.sum((earlier + offsets_in[None, :]) * matches, axis=1)
    blocks = factors[0]
    local_rows = jnp.zeros_like(targets) + my_row
    labels = jnp.stack(
        [jnp.ones_like(targets), targets // col_count, targets % col_count, slot_index, local_rows],
        axis=1,
    )
    row_ids = jnp.arange(row_count, dtype=jnp.int32)
    hold_places = jnp.arange(hold_count, dtype=jnp.int32)
    moved, moved_labels = bucket(blocks, labels, labels[:, 2], hold_places, col_count, hold_count)
    moved, moved_labels = (
        lax.all_to_all(moved, "col", split_axis=0, concat_axis=0, tiled=True),
        lax.all_to_all(
            as_sent(moved_labels), "col", split_axis=0, concat_axis=0, tiled=True
        ).astype(moved_labels.dtype),
    )
    moved, moved_labels = bucket(
        moved, moved_labels, moved_labels[:, 1], moved_labels[:, 3], row_count, CAP
    )
    moved, moved_labels = (
        lax.all_to_all(moved, "row", split_axis=0, concat_axis=0, tiled=True),
        lax.all_to_all(
            as_sent(moved_labels), "row", split_axis=0, concat_axis=0, tiled=True
        ).astype(moved_labels.dtype),
    )
    landed = jnp.sum(
        moved.reshape(row_count, CAP, block_width, block_width).astype(jnp.float32), axis=0
    )
    tags = jnp.sum(moved_labels.reshape(row_count, CAP, 5), axis=0)
    valid = tags[:, 0] > 0
    row_match = tags[:, 4][:, None] == row_ids[None, :]
    landed_sq = jnp.sum(landed * landed, axis=(1, 2))
    row_terms = jnp.sum(jnp.where(row_match & valid[:, None], landed_sq[:, None], 0.0), axis=0)
    layer_totals = lax.psum(row_terms, ("row", "col"))
    slot_totals = jnp.sum(jnp.where(row_match, layer_totals[None, :], 0.0), axis=1)
    scale = jnp.where(
        valid, 2.0 * jnp.sqrt(slot_totals / (col_count * hold_count * block_width)), 1.0
    )
    identity = jnp.eye(block_width, dtype=jnp.float32)
    moment = landed / scale[:, None, None]
    root_iter = jnp.broadcast_to(identity, landed.shape)
    for repeat in range(ITERS):
        step_mat = 1.25 * identity[None] - 0.25 * moment
        square_mat = jnp.einsum("bij,bjk->bik", step_mat, step_mat, precision=HIGH)
        fourth_mat = jnp.einsum("bij,bjk->bik", square_mat, square_mat, precision=HIGH)
        moment = jnp.einsum("bij,bjk->bik", fourth_mat, moment, precision=HIGH)
        root_iter = jnp.einsum("bij,bjk->bik", root_iter, step_mat, precision=HIGH)
    result = root_iter * (scale ** (-0.25))[:, None, None]
    result = jnp.where(valid[:, None, None], result, 0.0)
    return result[None]


def solution(mesh):
    return jax.shard_map(
        shards,
        mesh=mesh,
        in_specs=(P(("row", "col"), None, None, None), P(("row", "col"), None)),
        out_specs=P(("row", "col"), None, None, None),
        check_vma=False,
    )
```

profile of v0, /device:TPU:0, one launch (start us, length us, event | category | flops | bytes accessed | tf_op | source)
XLA Modules:
  0.0 472.4 jit_solution(13428662676525430576)
XLA Ops:
  0.0 0.7 fusion.33
  0.7 0.7 fusion.32
  1.5 0.7 copy.25
  2.2 0.7 fusion.35
  2.9 0.2 dynamic-update-slice
  3.1 42.0 %all-reduce = s32[1024]{0:T(1024)S(1)} all-reduce(s32[1024]{0:T(1024)S(1)} %dynamic-update-slice), channel_id=2, replica_groups=mesh['row'=4,'col'=8] {'row','col'}, use_global_device_ids=true, to_apply=%add | all-reduce | flops 1024 | bytes 8192
  45.1 0.1 reshape.123
  45.2 0.8 select_reduce_fusion.2
  46.0 0.1 copy.29
  46.2 0.1 stack.13
  46.3 0.7 fusion.24
  47.0 5.5 %all-to-all-start = ((s32[8,2,5]{2,1,0:T(2,128)}), s32[8,2,5]{2,1,0:T(2,128)S(1)}, u32[]{:S(2)}, u32[]{:S(2)}) async-start(s32[8,2,5]{2,1,0:T(2,128)} %bitcast.3), calls=%async_computation | async-start | bytes 16384 | tf_op jit(solution)/shard_map/all_to_all | solution.py:73
  52.5 2.3 copy.42
  54.8 5.5 %convolution_convert_fusion.1 = bf16[16,262144]{1,0:T(8,128)(2,1)} fusion(bf16[2,262144]{1,0:T(2,128)(2,1)S(1)} %bitcast.43, s32[2]{0:T(128)S(1)} %fusion.35), kind=kOutput, calls=%fused_computation.2 | convolution fusion | flops 20971552 | bytes 9437192 | tf_op jit(solution)/shard_map/dot_general | solution.py:37
  60.3 9.6 %copy.43 = bf16[2,8,512,512]{3,2,1,0:T(8,128)(2,1)} copy(bf16[2,8,512,512]{3,1,2,0:T(8,128)(2,1)} %bitcast.41) | data formatting | bytes 16777216
  69.9 0.0 all-to-all-done
  69.9 6.0 %all-to-all-start.2 = ((bf16[16,512,512]{2,1,0:T(8,128)(2,1)}), bf16[16,512,512]{2,1,0:T(8,128)(2,1)}, u32[]{:S(2)}, u32[]{:S(2)}) async-start(bf16[16,512,512]{2,1,0:T(8,128)(2,1)} %bitcast.40), calls=%async_computation.2 | async-start | bytes 16777216 | tf_op jit(solution)/shard_map/all_to_all | solution.py:72
  75.9 0.2 fusion.23
  76.1 0.1 broadcast_compare_fusion
  76.2 0.8 fusion.25
  77.0 180.2 %all-to-all-done.2 = bf16[16,512,512]{2,1,0:T(8,128)(2,1)} async-done(((bf16[16,512,512]{2,1,0:T(8,128)(2,1)}), bf16[16,512,512]{2,1,0:T(8,128)(2,1)}, u32[]{:S(2)}, u32[]{:S(2)}) %all-to-all-start.2) | async-done | bytes 8388640 | tf_op jit(solution)/shard_map/all_to_all | solution.py:72
  257.2 3.7 all-to-all-start.1
  260.8 11.3 %copy.44 = bf16[2,8,512,512]{3,1,2,0:T(8,128)(2,1)} copy(bf16[2,8,512,512]{3,2,1,0:T(8,128)(2,1)} %bitcast.15) | data formatting | bytes 16777216
  272.2 8.9 %convolution_convert_fusion = bf16[12,262144]{1,0:T(8,128)(2,1)} fusion(bf16[16,262144]{1,0:T(8,128)(2,1)} %bitcast.38, s32[16]{0:T(128)S(1)} %fusion.23), kind=kOutput, calls=%fused_computation.1 | convolution fusion | flops 103809216 | bytes 14680128 | tf_op jit(solution)/shard_map/dot_general | solution.py:37
  281.1 9.6 %copy.45 = bf16[2,8,512,512]{3,2,1,0:T(8,128)(2,1)} copy(bf16[2,8,512,512]{3,1,2,0:T(8,128)(2,1)} %bitcast.39) | data formatting | bytes 16777216
  290.7 5.8 %slice.23 = bf16[12,512,512]{2,1,0:T(8,128)(2,1)} slice(bf16[16,512,512]{2,1,0:T(8,128)(2,1)} %bitcast.42), slice={[0:12], [0:512], [0:512]} | slice | bytes 12582912 | tf_op jit(solution)/shard_map/reshape | solution.py:42
  296.5 0.0 all-to-all-done.1
  296.5 5.2 %all-to-all-start.3 = ((bf16[12,512,512]{2,1,0:T(8,128)(2,1)}), bf16[12,512,512]{2,1,0:T(8,128)(2,1)}, u32[]{:S(2)}, u32[]{:S(2)}) async-start(bf16[12,512,512]{2,1,0:T(8,128)(2,1)} %slice.23), calls=%async_computation.3 | async-start | bytes 12582912 | tf_op jit(solution)/shard_map/all_to_all | solution.py:81
  301.8 0.1 fusion.20
  301.9 0.2 slice_reduce_fusion
  302.1 0.1 fusion.31
  302.2 70.2 %all-to-all-done.3 = bf16[12,512,512]{2,1,0:T(8,128)(2,1)} async-done(((bf16[12,512,512]{2,1,0:T(8,128)(2,1)}), bf16[12,512,512]{2,1,0:T(8,128)(2,1)}, u32[]{:S(2)}, u32[]{:S(2)}) %all-to-all-start.3) | async-done | bytes 6291488 | tf_op jit(solution)/shard_map/all_to_all | solution.py:81
  372.4 4.1 convert_reduce_fusion
  376.5 0.0 copy-start
  376.5 1.7 copy-done
  378.2 0.4 multiply_reduce_fusion
  378.6 0.1 select_reduce_fusion.1
  378.7 0.1 fusion.21
  378.8 38.0 %psum.7 = f32[4]{0:T(128)S(1)} all-reduce(f32[4]{0:T(128)S(1)} %select_reduce_fusion.1), channel_id=1, replica_groups=mesh['row'=4,'col'=8] {'row','col'}, use_global_device_ids=true, to_apply=%region_9.10 | all-reduce | flops 4 | bytes 32 | tf_op jit(solution)/shard_map/psum | solution.py:94
  416.9 0.2 select_reduce_fusion
  417.1 8.8 %fusion.3 = f32[3,512,512]{2,1,0:T(8,128)S(1)} fusion(f32[512,512]{1,0:T(8,128)S(1)} %fusion.20, f32[3,512,512]{2,1,0:T(8,128)} %copy-done, f32[3]{0:T(128)S(1)} %get-tuple-element.38), kind=kOutput, calls=%fused_computation.11 | convolution fusion | flops 4834197504 | bytes 7340044 | tf_op jit(solution)/shard_map/bij,bjk->bik/dot_general | solution.py:104
  425.9 0.0 copy-start.1
  425.9 5.5 %fusion.43 = f32[3,512,512]{2,1,0:T(8,128)S(1)} fusion(f32[3,512,512]{2,1,0:T(8,128)S(1)} %fusion.3), kind=kOutput, calls=%fused_computation.77 | convolution fusion | flops 4831838208 | bytes 6291456 | tf_op jit(solution)/shard_map/bij,bjk->bik/dot_general | solution.py:105
  431.4 0.0 copy-done.1
  431.5 5.7 %fusion.42 = f32[3,512,512]{2,1,0:T(8,128)S(1)} fusion(f32[3,512,512]{2,1,0:T(8,128)S(1)} %fusion.43, f32[3,512,512]{2,1,0:T(8,128)S(1)} %copy-done.1, f32[3]{0:T(128)S(1)} %get-tuple-element.38), kind=kOutput, calls=%fused_computation.76 | convolution fusion | flops 4832624640 | bytes 9437196 | tf_op jit(solution)/shard_map/bij,bjk->bik/dot_general | solution.py:106
  437.1 5.5 %fusion.5 = f32[3,512,512]{2,1,0:T(8,128)S(1)} fusion(f32[3,512,512]{2,1,0:T(8,128)S(1)} %fusion.42, f32[512,512]{1,0:T(8,128)S(1)} %fusion.20), kind=kOutput, calls=%fused_computation.13 | convolution fusion | flops 4833411072 | bytes 7340032 | tf_op jit(solution)/shard_map/bij,bjk->bik/dot_general | solution.py:104
  442.7 5.7 %fusion.44 = f32[3,512,512]{2,1,0:T(8,128)S(1)} fusion(f32[3,512,512]{2,1,0:T(8,128)S(1)} %fusion.5), kind=kOutput, calls=%fused_computation.78 | convolution fusion | flops 4831838208 | bytes 6291456 | tf_op jit(solution)/shard_map/bij,bjk->bik/dot_general | solution.py:105
  448.4 5.3 %fusion.45 = f32[3,512,512]{2,1,0:T(8,128)S(1)} fusion(f32[3,512,512]{2,1,0:T(8,128)S(1)} %fusion.44, f32[3,512,512]{2,1,0:T(8,128)S(1)} %fusion.42), kind=kOutput, calls=%fused_computation.79 | convolution fusion | flops 4831838208 | bytes 9437184 | tf_op jit(solution)/shard_map/bij,bjk->bik/dot_general | solution.py:106
  453.7 5.5 %fusion.4 = f32[3,512,512]{2,1,0:T(8,128)S(1)} fusion(f32[512,512]{1,0:T(8,128)S(1)} %fusion.20, f32[512,512]{1,0:T(8,128)S(1)} %fusion.21, f32[3,512,512]{2,1,0:T(8,128)S(1)} %copy-done.1, f32[3]{0:T(128)S(1)} %get-tuple-element.38), kind=kOutput, calls=%fused_computation.12 | convolution fusion | flops 4834197504 | bytes 8388620 | tf_op jit(solution)/shard_map/bij,bjk->bik/dot_general | solution.py:107
  459.2 5.7 %fusion.6 = f32[3,512,512]{2,1,0:T(8,128)S(1)} fusion(f32[3,512,512]{2,1,0:T(8,128)S(1)} %fusion.4, f32[3,512,512]{2,1,0:T(8,128)S(1)} %fusion.42, f32[512,512]{1,0:T(8,128)S(1)} %fusion.20), kind=kOutput, calls=%fused_computation.14 | convolution fusion | flops 4833411072 | bytes 10485760 | tf_op jit(solution)/shard_map/bij,bjk->bik/dot_general | solution.py:107
  464.9 7.1 %select_bitcast_fusion = f32[1,3,512,512]{3,2,1,0:T(8,128)} fusion(f32[3,512,512]{2,1,0:T(8,128)S(1)} %fusion.6, f32[3,512,512]{2,1,0:T(8,128)S(1)} %fusion.45, f32[3]{0:T(128)S(1)} %get-tuple-element.37, f32[512,512]{1,0:T(8,128)S(1)} %fusion.20, pred[3]{0:T(512)(128)(4,1)S(1)} %fusion.31), kind=kOutput, calls=%fused_computation.4 | convolution fusion | flops 4834983936 | bytes 10485775 | tf_op jit(solution)/shard_map/bij,bjk->bik/dot_general | solution.py:107
  (10 shorter events, 0.1 us)
Async XLA Ops:
  47.0 22.9 %all-to-all-start = ((s32[8,2,5]{2,1,0:T(2,128)}), s32[8,2,5]{2,1,0:T(2,128)S(1)}, u32[]{:S(2)}, u32[]{:S(2)}) async-start(s32[8,2,5]{2,1,0:T(2,128)} %bitcast.3), calls=%async_computation | async-start | bytes 16384 | tf_op jit(solution)/shard_map/all_to_all | solution.py:73
  69.9 187.2 %all-to-all-start.2 = ((bf16[16,512,512]{2,1,0:T(8,128)(2,1)}), bf16[16,512,512]{2,1,0:T(8,128)(2,1)}, u32[]{:S(2)}, u32[]{:S(2)}) async-start(bf16[16,512,512]{2,1,0:T(8,128)(2,1)} %bitcast.40), calls=%async_computation.2 | async-start | bytes 16777216 | tf_op jit(solution)/shard_map/all_to_all | solution.py:72
  257.2 39.4 %all-to-all-start.1 = ((s32[4,3,5]{2,1,0:T(4,128)}), s32[4,3,5]{2,1,0:T(4,128)S(1)}, u32[]{:S(2)}, u32[]{:S(2)}) async-start(s32[4,3,5]{2,1,0:T(4,128)} %fusion.25), calls=%async_computation.1 | async-start | bytes 16384 | tf_op jit(solution)/shard_map/all_to_all | solution.py:82
  296.5 75.9 %all-to-all-start.3 = ((bf16[12,512,512]{2,1,0:T(8,128)(2,1)}), bf16[12,512,512]{2,1,0:T(8,128)(2,1)}, u32[]{:S(2)}, u32[]{:S(2)}) async-start(bf16[12,512,512]{2,1,0:T(8,128)(2,1)} %slice.23), calls=%async_computation.3 | async-start | bytes 12582912 | tf_op jit(solution)/shard_map/all_to_all | solution.py:81
  376.5 1.7 copy-start
  425.9 5.5 %copy-start.1 = (f32[3,512,512]{2,1,0:T(8,128)S(1)}, f32[3,512,512]{2,1,0:T(8,128)}, u32[]{:S(2)}) copy-start(f32[3,512,512]{2,1,0:T(8,128)} %copy-done) | copy-start | bytes 9437188
where the time goes:
time: 479 us; the launch traced here: 472 us
  waiting for transfers between devices  250 us (52%)
  blocking collectives  80 us (17%)
  matrix products  70.8 us (15%)
  local copies, waits for them, and re-layouts  41.8 us (9%)
  starting transfers between devices  20.4 us (4%)
  other arithmetic  8.44 us (2%)
    all_to_all x1, waiting for transfers between devices, shards(): lax.all_to_all(moved, 'col', split_axis=0, concat_axis=0, tiled=True)  180 us
    all_to_all x1, waiting for transfers between devices, shards(): lax.all_to_all(moved, 'row', split_axis=0, concat_axis=0, tiled=True)  70.2 us
    unnamed x1, blocking collectives  42 us
    psum x1, blocking collectives, shards(): layer_totals = lax.psum(row_terms, ('row', 'col'))  38 us
    unnamed x11, local copies, waits for them, and re-layouts  35.5 us
    dot_general x3, matrix products, shards(): root_iter = jnp.einsum('bij,bjk->bik', root_iter, step_mat, precision=HIGH)  18.3 us
    dot_general x2, matrix products, bucket(): jnp.dot(chooser.astype(jnp.bfloat16), blocks.reshape(item_total, block_wi...  14.4 us
    dot_general x2, matrix products, shards(): square_mat = jnp.einsum('bij,bjk->bik', step_mat, step_mat, precision=HIGH)  14.4 us
  transfers between devices with their start and end apart: 4, of which 2 were waited for; matrix products, arithmetic and copies ran while one was open for 12% of the time, Pallas kernels for 0%

commit v1 on v0

v1 whole, which is shorter than its diff:
```python
import functools
import jax
import jax.numpy as jnp
from jax import lax
from jax.experimental import pallas as pl
from jax.experimental.pallas import tpu as pltpu
from jax.sharding import PartitionSpec as P

CAP = 3
LANE = 128
INFO_ROWS = 8
AXES = ("row", "col")


def pack_kernel(pieces, target_ref, block_ref, packed_ref, info_ref):
    hold, width = block_ref.shape[1], block_ref.shape[2]
    half = width // 2
    depth = packed_ref.shape[2]
    row_ids = lax.broadcasted_iota(jnp.int32, (half, half), 0)
    col_ids = lax.broadcasted_iota(jnp.int32, (half, half), 1)
    info = jnp.zeros((INFO_ROWS, LANE), jnp.float32)
    info_row = lax.broadcasted_iota(jnp.int32, (INFO_ROWS, LANE), 0)
    info_col = lax.broadcasted_iota(jnp.int32, (INFO_ROWS, LANE), 1)
    square_sum = jnp.zeros((1, 1), jnp.float32)
    chunks = half // LANE
    for slot in range(hold):
        upper = block_ref[0, slot, :half, :half].astype(jnp.float32)
        corner = block_ref[0, slot, half:, :half]
        lower = block_ref[0, slot, half:, half:].astype(jnp.float32)
        wide = corner.astype(jnp.float32)
        folded = upper * upper + lower * lower + 2.0 * (wide * wide)
        square_sum = square_sum + jnp.sum(jnp.sum(folded, axis=0, keepdims=True), axis=1, keepdims=True)
        diagonal = jnp.sum(jnp.where(row_ids == col_ids, lower, 0.0), axis=0, keepdims=True)
        mixed = jnp.where(row_ids >= col_ids, upper, lower).astype(jnp.bfloat16)
        stripes = [corner[:, c * LANE:(c + 1) * LANE] for c in range(chunks)]
        stripes += [mixed[:, c * LANE:(c + 1) * LANE] for c in range(chunks)]
        per_stripe = half // depth
        for piece in range(pieces):
            stripe, place = piece // per_stripe, piece % per_stripe
            packed_ref[piece, slot] = stripes[stripe][place * depth:(place + 1) * depth]
        for c in range(chunks):
            line = diagonal[:, c * LANE:(c + 1) * LANE]
            info = jnp.where(info_row == slot * chunks + c, line, info)
    tail = info_row == hold * chunks
    info = jnp.where(tail & (info_col == 0), square_sum, info)
    for slot in range(hold):
        name = target_ref[slot, 0].astype(jnp.float32)
        info = jnp.where(tail & (info_col == 1 + slot), name, info)
    for piece in range(pieces):
        info_ref[piece] = info


def pack(factors, target, pieces):
    hold, width = factors.shape[1], factors.shape[2]
    depth = width * width // 2 // LANE // pieces
    return pl.pallas_call(
        functools.partial(pack_kernel, pieces),
        out_shape=(
            jax.ShapeDtypeStruct((pieces, hold, depth, LANE), jnp.bfloat16),
            jax.ShapeDtypeStruct((pieces, INFO_ROWS, LANE), jnp.float32),
        ),
        in_specs=[
            pl.BlockSpec(memory_space=pltpu.SMEM),
            pl.BlockSpec(memory_space=pltpu.VMEM),
        ],
        name="pack",
    )(target, factors)


def select_kernel(index_ref, pieces_ref, *out_refs):
    for slot, out_ref in enumerate(out_refs):
        for owner in range(out_ref.shape[0]):
            out_ref[owner] = pieces_ref[index_ref[slot, owner]]


def select(index, pieces):
    owners = index.shape[1]
    shape = jax.ShapeDtypeStruct((owners,) + pieces.shape[1:], pieces.dtype)
    return pl.pallas_call(
        select_kernel,
        out_shape=(shape,) * CAP,
        in_specs=[
            pl.BlockSpec(memory_space=pltpu.SMEM),
            pl.BlockSpec(memory_space=pltpu.VMEM),
        ],
        name="select",
    )(index, pieces)


def split(value):
    high = value.astype(jnp.bfloat16)
    return high, (value - high.astype(jnp.float32)).astype(jnp.bfloat16)


def dot(left, right):
    return jnp.dot(left, right, preferred_element_type=jnp.float32)


def product(left, right):
    return dot(
        jnp.concatenate([left[0], left[1], left[0]], axis=1),
        jnp.concatenate([right[0], right[0], right[1]], axis=0),
    )


def root_kernel(param_ref, packed_ref, diagonal_ref, *rest):
    out_ref, block_ref = rest[-2], rest[-1]
    width = out_ref.shape[1]
    half = width // 2
    chunks = half // LANE

    @pl.when(param_ref[0] > 0.0)
    def _():
        def square(first):
            return jnp.concatenate(
                [packed_ref[pl.ds((first + c) * half, half), :] for c in range(chunks)], axis=1
            )

        corner = square(0)
        mixed = square(chunks).astype(jnp.float32)
        turned = mixed.T
        row_ids = lax.broadcasted_iota(jnp.int32, (half, half), 0)
        col_ids = lax.broadcasted_iota(jnp.int32, (half, half), 1)
        upper = jnp.where(row_ids >= col_ids, mixed, turned)
        lower = jnp.where(row_ids < col_ids, mixed, turned)
        lower = jnp.where(row_ids == col_ids, diagonal_ref[...], lower)
        block_ref[:half, :half] = upper.astype(jnp.bfloat16)
        block_ref[:half, half:] = corner.astype(jnp.float32).T.astype(jnp.bfloat16)
        block_ref[half:, :half] = corner
        block_ref[half:, half:] = lower.astype(jnp.bfloat16)
        inverse = param_ref[1]
        block = block_ref[...]
        wide = block.astype(jnp.float32)
        rows = lax.broadcasted_iota(jnp.int32, (width, width), 0)
        cols = lax.broadcasted_iota(jnp.int32, (width, width), 1)
        eye = rows == cols
        step = jnp.where(eye, 1.25, 0.0) - (0.25 * inverse) * wide
        block_square = dot(block, block)
        step_square = (
            jnp.where(eye, 1.5625, 0.0)
            - (0.625 * inverse) * wide
            + (0.0625 * inverse * inverse) * block_square
        )
        parts = split(step_square)
        step_fourth = product(parts, parts)
        inner = split(step_square - 1.25 * step)
        pair = 1.25 * step + product(split(step_fourth), inner)
        pair_parts = split(pair)
        pair_square = split(product(pair_parts, pair_parts))
        pair_fourth = split(product(pair_square, pair_square))
        tail = dot(
            jnp.concatenate(pair_fourth, axis=1), jnp.concatenate([block, block], axis=0)
        )
        last = jnp.where(eye, 1.25, 0.0) - (0.25 * inverse) * tail
        out_ref[0] = product(pair_parts, split(last)) * param_ref[2]

    @pl.when(param_ref[0] <= 0.0)
    def _():
        out_ref[...] = jnp.zeros_like(out_ref)


def root(params, packed, diagonal, slot, width, held):
    shape = jax.ShapeDtypeStruct((CAP, width, width), jnp.float32)
    operands = [params, packed, diagonal]
    in_specs = [
        pl.BlockSpec(memory_space=pltpu.SMEM),
        pl.BlockSpec(memory_space=pltpu.VMEM),
        pl.BlockSpec(memory_space=pltpu.VMEM),
    ]
    aliases = {}
    if held is not None:
        operands.append(held)
        in_specs.append(pl.BlockSpec(memory_space=pl.ANY))
        aliases = {3: 0}
    return pl.pallas_call(
        root_kernel,
        grid=(1,),
        out_shape=shape,
        in_specs=in_specs,
        out_specs=pl.BlockSpec((1, width, width), lambda i: (slot, 0, 0)),
        scratch_shapes=[pltpu.VMEM((width, width), jnp.bfloat16)],
        input_output_aliases=aliases,
        cost_estimate=pl.CostEstimate(
            flops=36 * width ** 3, bytes_accessed=5 * width * width, transcendentals=0
        ),
        name="root",
    )(*operands)


def shards(factors, target):
    row_count, col_count = lax.axis_size("row"), lax.axis_size("col")
    devices = row_count * col_count
    hold, width = factors.shape[1], factors.shape[2]
    total = devices * hold
    me = lax.axis_index("row") * col_count + lax.axis_index("col")
    packed, info = pack(factors, target, devices)
    info = lax.all_to_all(info, AXES, split_axis=0, concat_axis=0, tiled=True)
    pieces = lax.all_to_all(packed, AXES, split_axis=0, concat_axis=0, tiled=True)
    lines = hold * width // 2 // LANE
    targets = info[:, lines, 1:1 + hold].reshape(total).astype(jnp.int32)
    squares = info[:, lines, 0].reshape(row_count, col_count)
    scales = 2.0 * jnp.sqrt(jnp.sum(squares, axis=1) / (col_count * hold * width))
    numbers = jnp.arange(total, dtype=jnp.int32)
    same = targets[:, None] == targets[None, :]
    slots = jnp.sum((same & (numbers[None, :] < numbers[:, None])).astype(jnp.int32), axis=1)
    places = jnp.arange(CAP * devices, dtype=jnp.int32)
    wanted = (slots * devices + targets)[None, :] == places[:, None]
    index = jnp.sum(jnp.where(wanted, numbers[None, :], 0), axis=1).reshape(CAP, devices)
    mine = (slots[None, :] == jnp.arange(CAP)[:, None]) & (targets[None, :] == me)
    valid = jnp.sum(mine.astype(jnp.float32), axis=1)
    per_block = jnp.repeat(scales, col_count * hold)
    scale = jnp.sum(jnp.where(mine, per_block[None, :], 0.0), axis=1)
    scale = jnp.where(valid > 0, scale, 1.0)
    params = jnp.stack([valid, 1.0 / scale, scale ** (-0.25)], axis=1)
    diagonals = info[:, :lines].reshape(total, width // 2)
    diagonal = jnp.sum(jnp.where(mine[:, :, None], diagonals[None], 0.0), axis=1)
    chosen = select(index, pieces.reshape((total,) + pieces.shape[2:]))
    held = None
    for slot in range(CAP):
        landed = lax.all_to_all(chosen[slot], AXES, split_axis=0, concat_axis=0, tiled=True)
        held = root(
            params[slot], landed.reshape(-1, LANE), diagonal[slot][None], slot, width, held
        )
    return held[None]


def solution(mesh):
    return jax.shard_map(
        shards,
        mesh=mesh,
        in_specs=(P(AXES, None, None, None), P(AXES, None)),
        out_specs=P(AXES, None, None, None),
        check_vma=False,
    )
```

time: 479 us -> 92.1 us (0.19)
  the two profiles are of different devices: /device:TPU:0 before, /device:TPU:2 now
where the time goes in v1:
time: 92.1 us; the launch traced here: 91.3 us
  waiting for transfers between devices  31.9 us (35%)
  Pallas kernels  27.1 us (29%)
  blocking collectives  13.3 us (14%)
  starting transfers between devices  12.4 us (13%)
  local copies, waits for them, and re-layouts  5.54 us (6%)
    pallas_call x3, Pallas kernels, root(): pl.pallas_call(root_kernel, grid=(1,), out_shape=shape, in_specs=in_specs...  22.7 us
    all_to_all x3, waiting for transfers between devices, shards(): lax.all_to_all(chosen[slot], AXES, split_axis=0, concat_axis=0, tiled=True)  18.1 us
    all_to_all x1, waiting for transfers between devices, shards(): lax.all_to_all(packed, AXES, split_axis=0, concat_axis=0, tiled=True)  13.8 us
    all_to_all x1, blocking collectives, shards(): info = lax.all_to_all(info, AXES, split_axis=0, concat_axis=0, tiled=True)  13.3 us
    all_to_all x3, starting transfers between devices, shards(): lax.all_to_all(chosen[slot], AXES, split_axis=0, concat_axis=0, tiled=True)  9.31 us
    all_to_all x1, starting transfers between devices, shards(): lax.all_to_all(packed, AXES, split_axis=0, concat_axis=0, tiled=True)  3.11 us
    unnamed x9, local copies, waits for them, and re-layouts  2.8 us
    pallas_call x1, Pallas kernels, pack(): pl.pallas_call(functools.partial(pack_kernel, pieces), out_shape=(jax.Sha...  2.43 us
  transfers between devices with their start and end apart: 4, of which 3 were waited for; matrix products, arithmetic and copies ran while one was open for 4% of the time, Pallas kernels for 16%

profile of v1, /device:TPU:2, one launch (start us, length us, event | category | flops | bytes accessed | tf_op | source)
XLA Modules:
  0.0 91.3 jit_solution(6649657450669780522)
XLA Ops:
  0.0 1.3 %copy.7.target_ref = s32[2,1]{1,0:T(2,128)} copy(s32[2,1]{0,1:T(1,128)} %param.3) | data formatting | bytes 16 | tf_op args[1]
  1.3 2.4 %pack.1 = (bf16[32,2,32,128]{3,2,1,0:T(8,128)(2,1)}, f32[32,8,128]{2,1,0:T(8,128)}) custom-call(s32[2,1]{1,0:T(2,128)} %copy.7.target_ref, bf16[1,2,512,512]{3,2,1,0:T(8,128)(2,1)} %block_ref.1), custom_call_target="tpu_custom_call" | custom-call | tf_op jit(solution)/shard_map/pack/pallas_call | solution.py:56
  3.7 13.3 %all_to_all.25 = f32[32,8,128]{2,1,0:T(8,128)S(1)} all-to-all(f32[32,8,128]{2,1,0:T(8,128)} %get-tuple-element.10), channel_id=1, replica_groups=mesh['row'=4,'col'=8] {'row','col'}, dimensions={0} | all-to-all | bytes 262144 | tf_op jit(solution)/shard_map/all_to_all | solution.py:197
  17.0 3.1 %all-to-all-start.1 = ((bf16[32,2,32,128]{3,2,1,0:T(8,128)(2,1)}), bf16[32,2,32,128]{3,2,1,0:T(8,128)(2,1)S(1)}, u32[]{:S(2)}, u32[]{:S(2)}) async-start(bf16[32,2,32,128]{3,2,1,0:T(8,128)(2,1)} %get-tuple-element.11), calls=%async_computation.1 | async-start | bytes 1048576 | tf_op jit(solution)/shard_map/all_to_all | solution.py:198
  20.2 0.3 slice_reduce_fusion
  20.5 0.1 reshape_squeeze.4
  20.6 0.1 fusion.1
  20.7 0.1 convert_element_type.27
  20.8 0.2 convert_reduce_fusion
  21.0 0.1 select_reduce_fusion.1
  21.1 0.7 reshape.98.index_ref
  21.8 0.1 reduce_sum.58
  21.9 13.8 %all-to-all-done.1 = bf16[32,2,32,128]{3,2,1,0:T(8,128)(2,1)S(1)} async-done(((bf16[32,2,32,128]{3,2,1,0:T(8,128)(2,1)}), bf16[32,2,32,128]{3,2,1,0:T(8,128)(2,1)S(1)}, u32[]{:S(2)}, u32[]{:S(2)}) %all-to-all-start.1) | async-done | bytes 524320 | tf_op jit(solution)/shard_map/all_to_all | solution.py:198
  35.7 0.0 copy-start
  35.7 0.8 copy-done
  36.5 2.0 %select.1 = (bf16[32,32,128]{2,1,0:T(8,128)(2,1)}, bf16[32,32,128]{2,1,0:T(8,128)(2,1)}, bf16[32,32,128]{2,1,0:T(8,128)(2,1)}) custom-call(s32[3,32]{1,0:T(4,128)} %reshape.98.index_ref, bf16[64,32,128]{2,1,0:T(8,128)(2,1)} %bitcast.17), custom_call_target="tpu_custom_call" | custom-call | tf_op jit(solution)/shard_map/select/pallas_call | solution.py:79
  38.5 3.3 %all-to-all-start.3 = ((bf16[32,32,128]{2,1,0:T(8,128)(2,1)}), bf16[32,32,128]{2,1,0:T(8,128)(2,1)S(1)}, u32[]{:S(2)}, u32[]{:S(2)}) async-start(bf16[32,32,128]{2,1,0:T(8,128)(2,1)} %get-tuple-element.13), calls=%async_computation.3 | async-start | bytes 524288 | tf_op jit(solution)/shard_map/all_to_all | solution.py:220
  41.8 0.1 broadcast_in_dim.67
  41.9 0.1 broadcast_in_dim.68
  42.0 0.1 convert_reduce_fusion.1
  42.1 9.7 %all-to-all-done.3 = bf16[32,32,128]{2,1,0:T(8,128)(2,1)S(1)} async-done(((bf16[32,32,128]{2,1,0:T(8,128)(2,1)}), bf16[32,32,128]{2,1,0:T(8,128)(2,1)S(1)}, u32[]{:S(2)}, u32[]{:S(2)}) %all-to-all-start.3) | async-done | bytes 262176 | tf_op jit(solution)/shard_map/all_to_all | solution.py:220
  51.8 0.0 copy-start.1
  51.8 3.0 %all-to-all-start.4 = ((bf16[32,32,128]{2,1,0:T(8,128)(2,1)}), bf16[32,32,128]{2,1,0:T(8,128)(2,1)S(1)}, u32[]{:S(2)}, u32[]{:S(2)}) async-start(bf16[32,32,128]{2,1,0:T(8,128)(2,1)} %get-tuple-element.14), calls=%async_computation.4 | async-start | bytes 524288 | tf_op jit(solution)/shard_map/all_to_all | solution.py:220
  54.9 0.8 slice_reduce_fusion.1
  55.7 0.1 select_reduce_fusion
  55.8 0.6 fusion.4
  56.4 8.5 %all-to-all-done.4 = bf16[32,32,128]{2,1,0:T(8,128)(2,1)S(1)} async-done(((bf16[32,32,128]{2,1,0:T(8,128)(2,1)}), bf16[32,32,128]{2,1,0:T(8,128)(2,1)S(1)}, u32[]{:S(2)}, u32[]{:S(2)}) %all-to-all-start.4) | async-done | bytes 262176 | tf_op jit(solution)/shard_map/all_to_all | solution.py:220
  64.8 0.0 copy-start.2
  64.8 3.0 %all-to-all-start.2 = ((bf16[32,32,128]{2,1,0:T(8,128)(2,1)}), bf16[32,32,128]{2,1,0:T(8,128)(2,1)S(1)}, u32[]{:S(2)}, u32[]{:S(2)}) async-start(bf16[32,32,128]{2,1,0:T(8,128)(2,1)} %get-tuple-element.12), calls=%async_computation.2 | async-start | bytes 524288 | tf_op jit(solution)/shard_map/all_to_all | solution.py:220
  67.9 0.0 copy-done.2
  67.9 7.5 %root.3.rest_0_ = f32[3,512,512]{2,1,0:T(8,128)} custom-call(f32[3]{0:T(128)} %get-tuple-element.15.param_ref, bf16[1024,128]{1,0:T(8,128)(2,1)} %bitcast.19, f32[1,256]{1,0:T(1,128)} %get-tuple-element.21.diagonal_ref), custom_call_target="tpu_custom_call" | custom-call | flops 4831838208 | bytes 1310720 | tf_op jit(solution)/shard_map/root/pallas_call | solution.py:175
  75.4 0.0 copy-done.1
  75.4 7.5 %root.4.rest_0_ = f32[3,512,512]{2,1,0:T(8,128)} custom-call(f32[3]{0:T(128)} %get-tuple-element.16.param_ref, bf16[1024,128]{1,0:T(8,128)(2,1)} %bitcast.18, f32[1,256]{1,0:T(1,128)} %get-tuple-element.22.diagonal_ref, f32[3,512,512]{2,1,0:T(8,128)} %root.3.rest_0_), custom_call_target="tpu_custom_call", output_to_operand_aliasing={{}: (3, {})} | custom-call | flops 4831838208 | bytes 1310720 | tf_op jit(solution)/shard_map/root/pallas_call | solution.py:175
  82.9 0.0 all-to-all-done.2
  82.9 0.0 copy-start.3
  82.9 0.7 copy-done.3
  83.6 7.7 %root.5 = f32[3,512,512]{2,1,0:T(8,128)} custom-call(f32[3]{0:T(128)} %get-tuple-element.17.param_ref, bf16[1024,128]{1,0:T(8,128)(2,1)} %bitcast.20, f32[1,256]{1,0:T(1,128)} %get-tuple-element.23.diagonal_ref, f32[3,512,512]{2,1,0:T(8,128)} %root.4.rest_0_), custom_call_target="tpu_custom_call", output_to_operand_aliasing={{}: (3, {})} | custom-call | flops 4831838208 | bytes 1310720 | tf_op jit(solution)/shard_map/root/pallas_call | solution.py:175
  (7 shorter events, 0.1 us)
Async XLA Ops:
  17.0 18.7 %all-to-all-start.1 = ((bf16[32,2,32,128]{3,2,1,0:T(8,128)(2,1)}), bf16[32,2,32,128]{3,2,1,0:T(8,128)(2,1)S(1)}, u32[]{:S(2)}, u32[]{:S(2)}) async-start(bf16[32,2,32,128]{3,2,1,0:T(8,128)(2,1)} %get-tuple-element.11), calls=%async_computation.1 | async-start | bytes 1048576 | tf_op jit(solution)/shard_map/all_to_all | solution.py:198
  35.7 0.8 copy-start
  38.5 13.3 %all-to-all-start.3 = ((bf16[32,32,128]{2,1,0:T(8,128)(2,1)}), bf16[32,32,128]{2,1,0:T(8,128)(2,1)S(1)}, u32[]{:S(2)}, u32[]{:S(2)}) async-start(bf16[32,32,128]{2,1,0:T(8,128)(2,1)} %get-tuple-element.13), calls=%async_computation.3 | async-start | bytes 524288 | tf_op jit(solution)/shard_map/all_to_all | solution.py:220
  51.8 23.6 %copy-start.1 = (bf16[32,32,128]{2,1,0:T(8,128)(2,1)}, bf16[32,32,128]{2,1,0:T(8,128)(2,1)S(1)}, u32[]{:S(2)}) copy-start(bf16[32,32,128]{2,1,0:T(8,128)(2,1)S(1)} %all-to-all-done.3) | copy-start | bytes 786436
  51.8 13.0 %all-to-all-start.4 = ((bf16[32,32,128]{2,1,0:T(8,128)(2,1)}), bf16[32,32,128]{2,1,0:T(8,128)(2,1)S(1)}, u32[]{:S(2)}, u32[]{:S(2)}) async-start(bf16[32,32,128]{2,1,0:T(8,128)(2,1)} %get-tuple-element.14), calls=%async_computation.4 | async-start | bytes 524288 | tf_op jit(solution)/shard_map/all_to_all | solution.py:220
  64.8 3.0 %copy-start.2 = (bf16[32,32,128]{2,1,0:T(8,128)(2,1)}, bf16[32,32,128]{2,1,0:T(8,128)(2,1)S(1)}, u32[]{:S(2)}) copy-start(bf16[32,32,128]{2,1,0:T(8,128)(2,1)S(1)} %all-to-all-done.4) | copy-start | bytes 786436
  64.8 18.0 %all-to-all-start.2 = ((bf16[32,32,128]{2,1,0:T(8,128)(2,1)}), bf16[32,32,128]{2,1,0:T(8,128)(2,1)S(1)}, u32[]{:S(2)}, u32[]{:S(2)}) async-start(bf16[32,32,128]{2,1,0:T(8,128)(2,1)} %get-tuple-element.12), calls=%async_computation.2 | async-start | bytes 524288 | tf_op jit(solution)/shard_map/all_to_all | solution.py:220
  82.9 0.7 copy-start.3

commit v2 on v1

v2 whole, which is shorter than its diff:
```python
import functools
import jax
import jax.numpy as jnp
from jax import lax
from jax.experimental import pallas as pl
from jax.experimental.pallas import tpu as pltpu
from jax.sharding import PartitionSpec as P

CAP = 3
LANE = 128
INFO_ROWS = 8
SQUARE_PARTS = 3
NAME_PARTS = 2
EARLY = 2
AXES = ("row", "col")


def parts_of(value, count):
    parts = []
    for _ in range(count):
        part = value.astype(jnp.bfloat16)
        parts.append(part)
        value = value - part.astype(jnp.float32)
    return parts


def pack_kernel(pieces, target_ref, block_ref, packed_ref):
    hold, width = block_ref.shape[1], block_ref.shape[2]
    half = width // 2
    depth = (packed_ref.shape[1] - INFO_ROWS) // hold
    row_ids = lax.broadcasted_iota(jnp.int32, (half, half), 0)
    col_ids = lax.broadcasted_iota(jnp.int32, (half, half), 1)
    info = jnp.zeros((INFO_ROWS, LANE), jnp.float32)
    info_row = lax.broadcasted_iota(jnp.int32, (INFO_ROWS, LANE), 0)
    info_col = lax.broadcasted_iota(jnp.int32, (INFO_ROWS, LANE), 1)
    square_sum = jnp.zeros((1, 1), jnp.float32)
    chunks = half // LANE
    for slot in range(hold):
        upper = block_ref[0, slot, :half, :half].astype(jnp.float32)
        corner = block_ref[0, slot, half:, :half]
        lower = block_ref[0, slot, half:, half:].astype(jnp.float32)
        wide = corner.astype(jnp.float32)
        folded = upper * upper + lower * lower + 2.0 * (wide * wide)
        square_sum = square_sum + jnp.sum(jnp.sum(folded, axis=0, keepdims=True), axis=1, keepdims=True)
        diagonal = jnp.sum(jnp.where(row_ids == col_ids, lower, 0.0), axis=0, keepdims=True)
        mixed = jnp.where(row_ids >= col_ids, upper, lower).astype(jnp.bfloat16)
        stripes = [corner[:, c * LANE:(c + 1) * LANE] for c in range(chunks)]
        stripes += [mixed[:, c * LANE:(c + 1) * LANE] for c in range(chunks)]
        per_stripe = half // depth
        for piece in range(pieces):
            stripe, place = piece // per_stripe, piece % per_stripe
            packed_ref[piece, slot * depth:(slot + 1) * depth] = (
                stripes[stripe][place * depth:(place + 1) * depth]
            )
        for c in range(chunks):
            line = diagonal[:, c * LANE:(c + 1) * LANE]
            info = jnp.where(info_row == slot * chunks + c, line, info)
    tail = info_row == hold * chunks
    values = parts_of(square_sum, SQUARE_PARTS)
    for slot in range(hold):
        name = jnp.zeros((1, 1), jnp.float32) + target_ref[slot, 0].astype(jnp.float32)
        values += parts_of(name, NAME_PARTS)
    for place, value in enumerate(values):
        info = jnp.where(tail & (info_col == place), value.astype(jnp.float32), info)
    info = info.astype(jnp.bfloat16)
    for piece in range(pieces):
        packed_ref[piece, hold * depth:] = info


def pack(factors, target, pieces):
    hold, width = factors.shape[1], factors.shape[2]
    depth = width * width // 2 // LANE // pieces
    return pl.pallas_call(
        functools.partial(pack_kernel, pieces),
        out_shape=jax.ShapeDtypeStruct((pieces, hold * depth + INFO_ROWS, LANE), jnp.bfloat16),
        in_specs=[
            pl.BlockSpec(memory_space=pltpu.SMEM),
            pl.BlockSpec(memory_space=pltpu.VMEM),
        ],
        name="pack",
    )(target, factors)


def select_kernel(hold, index_ref, pieces_ref, early_ref, late_ref):
    early, depth = early_ref.shape[1], early_ref.shape[2]
    for owner in range(early_ref.shape[0]):
        for slot in range(CAP):
            block = index_ref[slot, owner]
            first = pl.multiple_of((block % hold) * depth, depth)
            piece = pieces_ref[block // hold, pl.ds(first, depth), :]
            if slot < early:
                early_ref[owner, slot] = piece
            else:
                late_ref[owner, slot - early] = piece


def select(index, pieces, hold):
    owners = index.shape[1]
    depth = (pieces.shape[1] - INFO_ROWS) // hold
    return pl.pallas_call(
        functools.partial(select_kernel, hold),
        out_shape=(
            jax.ShapeDtypeStruct((owners, EARLY, depth, LANE), pieces.dtype),
            jax.ShapeDtypeStruct((owners, CAP - EARLY, depth, LANE), pieces.dtype),
        ),
        in_specs=[
            pl.BlockSpec(memory_space=pltpu.SMEM),
            pl.BlockSpec(memory_space=pltpu.VMEM),
        ],
        name="select",
    )(index, pieces)


def split(value):
    high = value.astype(jnp.bfloat16)
    return high, (value - high.astype(jnp.float32)).astype(jnp.bfloat16)


def dot(left, right):
    return jnp.dot(left, right, preferred_element_type=jnp.float32)


def product(left, right):
    return dot(
        jnp.concatenate([left[0], left[1], left[0]], axis=1),
        jnp.concatenate([right[0], right[0], right[1]], axis=0),
    )


def root_kernel(first, param_ref, packed_ref, diagonal_ref, *rest):
    out_ref, block_ref = rest[-2], rest[-1]
    width = out_ref.shape[1]
    half = width // 2
    chunks = half // LANE
    owners, depth = packed_ref.shape[0], packed_ref.shape[2]
    here = pl.program_id(0)
    slot = first + here
    lines = packed_ref[:, here].reshape(owners * depth, LANE)

    def square(place):
        return jnp.concatenate(
            [lines[(place + c) * half:(place + c + 1) * half] for c in range(chunks)], axis=1
        )

    corner = square(0)
    mixed = square(chunks).astype(jnp.float32)
    turned = mixed.T
    row_ids = lax.broadcasted_iota(jnp.int32, (half, half), 0)
    col_ids = lax.broadcasted_iota(jnp.int32, (half, half), 1)
    upper = jnp.where(row_ids >= col_ids, mixed, turned)
    lower = jnp.where(row_ids < col_ids, mixed, turned)
    lower = jnp.where(row_ids == col_ids, diagonal_ref[pl.ds(slot, 1), :], lower)
    block_ref[:half, :half] = upper.astype(jnp.bfloat16)
    block_ref[:half, half:] = corner.astype(jnp.float32).T.astype(jnp.bfloat16)
    block_ref[half:, :half] = corner
    block_ref[half:, half:] = lower.astype(jnp.bfloat16)
    inverse = param_ref[slot, 1]
    block = block_ref[...]
    wide = block.astype(jnp.float32)
    rows = lax.broadcasted_iota(jnp.int32, (width, width), 0)
    cols = lax.broadcasted_iota(jnp.int32, (width, width), 1)
    eye = rows == cols
    step = jnp.where(eye, 1.25, 0.0) - (0.25 * inverse) * wide
    block_square = dot(block, block)
    step_square = (
        jnp.where(eye, 1.5625, 0.0)
        - (0.625 * inverse) * wide
        + (0.0625 * inverse * inverse) * block_square
    )
    parts = split(step_square)
    step_fourth = product(parts, parts)
    inner = split(step_square - 1.25 * step)
    pair = 1.25 * step + product(split(step_fourth), inner)
    pair_parts = split(pair)
    pair_square = split(product(pair_parts, pair_parts))
    pair_fourth = split(product(pair_square, pair_square))
    tail = dot(jnp.concatenate(pair_fourth, axis=1), jnp.concatenate([block, block], axis=0))
    last = jnp.where(eye, 1.25, 0.0) - (0.25 * inverse) * tail
    result = product(pair_parts, split(last)) * param_ref[slot, 2]
    out_ref[0] = jnp.where(param_ref[slot, 0] > 0.0, result, 0.0)


def root(params, packed, diagonal, first, width, held):
    count = packed.shape[1]
    operands = [params, packed, diagonal]
    in_specs = [
        pl.BlockSpec(memory_space=pltpu.SMEM),
        pl.BlockSpec(memory_space=pltpu.VMEM),
        pl.BlockSpec(memory_space=pltpu.VMEM),
    ]
    aliases = {}
    if held is not None:
        operands.append(held)
        in_specs.append(pl.BlockSpec(memory_space=pl.ANY))
        aliases = {3: 0}
    return pl.pallas_call(
        functools.partial(root_kernel, first),
        grid=(count,),
        out_shape=jax.ShapeDtypeStruct((CAP, width, width), jnp.float32),
        in_specs=in_specs,
        out_specs=pl.BlockSpec((1, width, width), lambda i: (first + i, 0, 0)),
        scratch_shapes=[pltpu.VMEM((width, width), jnp.bfloat16)],
        input_output_aliases=aliases,
        cost_estimate=pl.CostEstimate(
            flops=36 * count * width ** 3,
            bytes_accessed=5 * count * width * width,
            transcendentals=0,
        ),
        name="root",
    )(*operands)


def shards(factors, target):
    row_count, col_count = lax.axis_size("row"), lax.axis_size("col")
    devices = row_count * col_count
    hold, width = factors.shape[1], factors.shape[2]
    total = devices * hold
    me = lax.axis_index("row") * col_count + lax.axis_index("col")
    packed = pack(factors, target, devices)
    pieces = lax.all_to_all(packed, AXES, split_axis=0, concat_axis=0, tiled=True)
    lines = hold * width // 2 // LANE
    info = pieces[:, -INFO_ROWS:].astype(jnp.float32)
    tail = info[:, lines]
    named = tail[:, SQUARE_PARTS:SQUARE_PARTS + hold * NAME_PARTS]
    targets = jnp.sum(named.reshape(total, NAME_PARTS), axis=1).astype(jnp.int32)
    squares = jnp.sum(tail[:, :SQUARE_PARTS], axis=1).reshape(row_count, col_count)
    scales = 2.0 * jnp.sqrt(jnp.sum(squares, axis=1) / (col_count * hold * width))
    numbers = jnp.arange(total, dtype=jnp.int32)
    same = targets[:, None] == targets[None, :]
    slots = jnp.sum((same & (numbers[None, :] < numbers[:, None])).astype(jnp.int32), axis=1)
    places = jnp.arange(CAP * devices, dtype=jnp.int32)
    wanted = (slots * devices + targets)[None, :] == places[:, None]
    index = jnp.sum(jnp.where(wanted, numbers[None, :], 0), axis=1).reshape(CAP, devices)
    mine = (slots[None, :] == jnp.arange(CAP)[:, None]) & (targets[None, :] == me)
    valid = jnp.sum(mine.astype(jnp.float32), axis=1)
    per_block = jnp.repeat(scales, col_count * hold)
    scale = jnp.sum(jnp.where(mine, per_block[None, :], 0.0), axis=1)
    scale = jnp.where(valid > 0, scale, 1.0)
    params = jnp.stack([valid, 1.0 / scale, scale ** (-0.25)], axis=1)
    diagonals = info[:, :lines].reshape(total, width // 2)
    diagonal = jnp.sum(jnp.where(mine[:, :, None], diagonals[None], 0.0), axis=1)
    early, late = select(index, pieces, hold)
    early = lax.all_to_all(early, AXES, split_axis=0, concat_axis=0, tiled=True)
    late = lax.all_to_all(late, AXES, split_axis=0, concat_axis=0, tiled=True)
    held = root(params, early, diagonal, 0, width, None)
    return root(params, late, diagonal, EARLY, width, held)[None]


def solution(mesh):
    return jax.shard_map(
        shards,
        mesh=mesh,
        in_specs=(P(AXES, None, None, None), P(AXES, None)),
        out_specs=P(AXES, None, None, None),
        check_vma=False,
    )
```

time: 92.1 us -> 76.3 us (0.83)
  the two profiles are of different devices: /device:TPU:2 before, /device:TPU:0 now
where the time goes in v2:
time: 76.3 us; the launch traced here: 75.9 us
  waiting for transfers between devices  32 us (42%)
  Pallas kernels  25.8 us (34%)
  starting transfers between devices  12.5 us (16%)
  local copies, waits for them, and re-layouts  3.34 us (4%)
  other arithmetic  2.18 us (3%)
    pallas_call x2, Pallas kernels, root(): pl.pallas_call(functools.partial(root_kernel, first), grid=(count,), out_...  20.7 us
    all_to_all x1, waiting for transfers between devices, shards(): lax.all_to_all(packed, AXES, split_axis=0, concat_axis=0, tiled=True)  17.6 us
    all_to_all x1, waiting for transfers between devices, shards(): early = lax.all_to_all(early, AXES, split_axis=0, concat_axis=0, tiled=True)  14.3 us
    all_to_all x1, starting transfers between devices, shards(): lax.all_to_all(packed, AXES, split_axis=0, concat_axis=0, tiled=True)  7.33 us
    pallas_call x1, Pallas kernels, select(): pl.pallas_call(functools.partial(select_kernel, hold), out_shape=(jax.Sha...  2.61 us
    all_to_all x1, starting transfers between devices, shards(): early = lax.all_to_all(early, AXES, split_axis=0, concat_axis=0, tiled=True)  2.6 us
    all_to_all x1, starting transfers between devices, shards(): late = lax.all_to_all(late, AXES, split_axis=0, concat_axis=0, tiled=True)  2.58 us
    pallas_call x1, Pallas kernels, pack(): pl.pallas_call(functools.partial(pack_kernel, pieces), out_shape=jax.Shap...  2.46 us
  transfers between devices with their start and end apart: 3, of which 2 were waited for; matrix products, arithmetic and copies ran while one was open for 2% of the time, Pallas kernels for 17%

profile of v2, /device:TPU:0, one launch (start us, length us, event | category | flops | bytes accessed | tf_op | source)
XLA Modules:
  0.0 75.9 jit_solution(2329732445336152580)
XLA Ops:
  0.0 1.3 %copy.12.target_ref = s32[2,1]{1,0:T(2,128)} copy(s32[2,1]{0,1:T(1,128)} %param.3) | data formatting | bytes 16 | tf_op args[1]
  1.3 2.5 %pack.1 = bf16[32,72,128]{2,1,0:T(8,128)(2,1)} custom-call(s32[2,1]{1,0:T(2,128)} %copy.12.target_ref, bf16[1,2,512,512]{3,2,1,0:T(8,128)(2,1)} %block_ref.1), custom_call_target="tpu_custom_call" | custom-call | tf_op jit(solution)/shard_map/pack/pallas_call | solution.py:73
  3.8 7.3 %all-to-all-start = ((bf16[32,72,128]{2,1,0:T(8,128)(2,1)}), bf16[32,72,128]{2,1,0:T(8,128)(2,1)S(1)}, u32[]{:S(2)}, u32[]{:S(2)}) async-start(bf16[32,72,128]{2,1,0:T(8,128)(2,1)} %pack.1), calls=%async_computation | async-start | bytes 1179648 | tf_op jit(solution)/shard_map/all_to_all | solution.py:220
  11.1 17.6 %all-to-all-done.pieces_ref = bf16[32,72,128]{2,1,0:T(8,128)(2,1)S(1)} async-done(((bf16[32,72,128]{2,1,0:T(8,128)(2,1)}), bf16[32,72,128]{2,1,0:T(8,128)(2,1)S(1)}, u32[]{:S(2)}, u32[]{:S(2)}) %all-to-all-start) | async-done | bytes 589856 | tf_op jit(solution)/shard_map/all_to_all | solution.py:220
  28.8 0.0 copy-start
  28.8 0.1 slice_reduce_fusion
  28.9 0.1 slice.22
  29.0 0.1 reshape.86
  29.1 0.1 reshape.85
  29.2 0.1 reduce_sum.78
  29.3 0.1 reduce_sum.74
  29.4 0.2 convert_reduce_fusion
  29.6 0.1 select_reduce_fusion.1
  29.7 0.7 reshape.87.index_ref
  30.4 0.0 copy-done
  30.4 2.6 %select.1 = (bf16[32,2,32,128]{3,2,1,0:T(8,128)(2,1)}, bf16[32,1,32,128]{3,2,1,0:T(8,128)(2,1)}) custom-call(s32[3,32]{1,0:T(4,128)} %reshape.87.index_ref, bf16[32,72,128]{2,1,0:T(8,128)(2,1)} %copy-done), custom_call_target="tpu_custom_call" | custom-call | tf_op jit(solution)/shard_map/select/pallas_call | solution.py:100
  33.0 2.6 %all-to-all-start.2 = ((bf16[32,2,32,128]{3,2,1,0:T(8,128)(2,1)}), bf16[32,2,32,128]{3,2,1,0:T(8,128)(2,1)S(1)}, u32[]{:S(2)}, u32[]{:S(2)}) async-start(bf16[32,2,32,128]{3,2,1,0:T(8,128)(2,1)} %get-tuple-element.8), calls=%async_computation.2 | async-start | bytes 1048576 | tf_op jit(solution)/shard_map/all_to_all | solution.py:243
  35.7 0.1 broadcast_in_dim.67
  35.7 0.1 broadcast_in_dim.68
  35.8 0.2 convert_reduce_fusion.1
  36.0 0.1 copy.15
  36.1 0.1 copy.14
  36.2 0.7 pad_maximum_fusion.param_ref
  36.9 0.7 select_reduce_fusion.diagonal_ref
  37.5 14.3 %all-to-all-done.2.packed_ref = bf16[32,2,32,128]{3,2,1,0:T(8,128)(2,1)S(1)} async-done(((bf16[32,2,32,128]{3,2,1,0:T(8,128)(2,1)}), bf16[32,2,32,128]{3,2,1,0:T(8,128)(2,1)S(1)}, u32[]{:S(2)}, u32[]{:S(2)}) %all-to-all-start.2) | async-done | bytes 524320 | tf_op jit(solution)/shard_map/all_to_all | solution.py:243
  51.9 0.0 copy-start.1
  51.9 2.6 %all-to-all-start.1 = ((bf16[32,1,32,128]{3,2,1,0:T(8,128)(2,1)}), bf16[32,1,32,128]{3,2,1,0:T(8,128)(2,1)S(1)}, u32[]{:S(2)}, u32[]{:S(2)}) async-start(bf16[32,1,32,128]{3,2,1,0:T(8,128)(2,1)} %get-tuple-element.7), calls=%async_computation.1 | async-start | bytes 524288 | tf_op jit(solution)/shard_map/all_to_all | solution.py:244
  54.5 0.0 copy-done.1
  54.5 13.2 %root.2.rest_0_ = f32[3,512,512]{2,1,0:T(8,128)} custom-call(f32[3,3]{1,0:T(4,128)} %pad_maximum_fusion.param_ref, bf16[32,2,32,128]{3,2,1,0:T(8,128)(2,1)} %copy-done.1, f32[3,256]{1,0:T(4,128)} %select_reduce_fusion.diagonal_ref), custom_call_target="tpu_custom_call" | custom-call | flops 9663676416 | bytes 2621440 | tf_op jit(solution)/shard_map/root/pallas_call | solution.py:196
  67.7 0.0 all-to-all-done.1.packed_ref
  67.7 0.0 copy-start.2
  67.7 0.7 copy-done.2
  68.4 7.5 %root.3 = f32[3,512,512]{2,1,0:T(8,128)} custom-call(f32[3,3]{1,0:T(4,128)} %pad_maximum_fusion.param_ref, bf16[32,1,32,128]{3,2,1,0:T(8,128)(2,1)} %copy-done.2, f32[3,256]{1,0:T(4,128)} %select_reduce_fusion.diagonal_ref, f32[3,512,512]{2,1,0:T(8,128)} %root.2.rest_0_), custom_call_target="tpu_custom_call", output_to_operand_aliasing={{}: (3, {})} | custom-call | flops 4831838208 | bytes 1310720 | tf_op jit(solution)/shard_map/root/pallas_call | solution.py:196
  (9 shorter events, 0.1 us)
Async XLA Ops:
  3.8 25.0 %all-to-all-start = ((bf16[32,72,128]{2,1,0:T(8,128)(2,1)}), bf16[32,72,128]{2,1,0:T(8,128)(2,1)S(1)}, u32[]{:S(2)}, u32[]{:S(2)}) async-start(bf16[32,72,128]{2,1,0:T(8,128)(2,1)} %pack.1), calls=%async_computation | async-start | bytes 1179648 | tf_op jit(solution)/shard_map/all_to_all | solution.py:220
  28.8 1.7 %copy-start = (bf16[32,72,128]{2,1,0:T(8,128)(2,1)}, bf16[32,72,128]{2,1,0:T(8,128)(2,1)S(1)}, u32[]{:S(2)}) copy-start(bf16[32,72,128]{2,1,0:T(8,128)(2,1)S(1)} %all-to-all-done.pieces_ref) | copy-start | bytes 1769476
  33.0 18.8 %all-to-all-start.2 = ((bf16[32,2,32,128]{3,2,1,0:T(8,128)(2,1)}), bf16[32,2,32,128]{3,2,1,0:T(8,128)(2,1)S(1)}, u32[]{:S(2)}, u32[]{:S(2)}) async-start(bf16[32,2,32,128]{3,2,1,0:T(8,128)(2,1)} %get-tuple-element.8), calls=%async_computation.2 | async-start | bytes 1048576 | tf_op jit(solution)/shard_map/all_to_all | solution.py:243
  51.9 2.6 %copy-start.1 = (bf16[32,2,32,128]{3,2,1,0:T(8,128)(2,1)}, bf16[32,2,32,128]{3,2,1,0:T(8,128)(2,1)S(1)}, u32[]{:S(2)}) copy-start(bf16[32,2,32,128]{3,2,1,0:T(8,128)(2,1)S(1)} %all-to-all-done.2.packed_ref) | copy-start | bytes 1572868
  51.9 15.8 %all-to-all-start.1 = ((bf16[32,1,32,128]{3,2,1,0:T(8,128)(2,1)}), bf16[32,1,32,128]{3,2,1,0:T(8,128)(2,1)S(1)}, u32[]{:S(2)}, u32[]{:S(2)}) async-start(bf16[32,1,32,128]{3,2,1,0:T(8,128)(2,1)} %get-tuple-element.7), calls=%async_computation.1 | async-start | bytes 524288 | tf_op jit(solution)/shard_map/all_to_all | solution.py:244
  67.7 0.7 copy-start.2

commit v3 on v2

v3 whole, which is shorter than its diff:
```python
import functools
import jax
import jax.numpy as jnp
from jax import lax
from jax.experimental import pallas as pl
from jax.experimental.pallas import tpu as pltpu
from jax.sharding import PartitionSpec as P

CAP = 3
LANE = 128
INFO_ROWS = 8
SQUARE_PARTS = 3
NAME_PARTS = 2
EARLY = 2
AXES = ("row", "col")


def parts_of(value, count):
    parts = []
    for _ in range(count):
        part = value.astype(jnp.bfloat16)
        parts.append(part)
        value = value - part.astype(jnp.float32)
    return parts


def pack_kernel(pieces, target_ref, block_ref, packed_ref):
    hold, width = block_ref.shape[1], block_ref.shape[2]
    half = width // 2
    depth = (packed_ref.shape[1] - INFO_ROWS) // hold
    row_ids = lax.broadcasted_iota(jnp.int32, (half, half), 0)
    col_ids = lax.broadcasted_iota(jnp.int32, (half, half), 1)
    info = jnp.zeros((INFO_ROWS, LANE), jnp.float32)
    info_row = lax.broadcasted_iota(jnp.int32, (INFO_ROWS, LANE), 0)
    info_col = lax.broadcasted_iota(jnp.int32, (INFO_ROWS, LANE), 1)
    square_sum = jnp.zeros((1, 1), jnp.float32)
    chunks = half // LANE
    for slot in range(hold):
        upper = block_ref[0, slot, :half, :half].astype(jnp.float32)
        corner = block_ref[0, slot, half:, :half]
        lower = block_ref[0, slot, half:, half:].astype(jnp.float32)
        wide = corner.astype(jnp.float32)
        folded = upper * upper + lower * lower + 2.0 * (wide * wide)
        square_sum = square_sum + jnp.sum(jnp.sum(folded, axis=0, keepdims=True), axis=1, keepdims=True)
        diagonal = jnp.sum(jnp.where(row_ids == col_ids, lower, 0.0), axis=0, keepdims=True)
        mixed = jnp.where(row_ids >= col_ids, upper, lower).astype(jnp.bfloat16)
        stripes = [corner[:, c * LANE:(c + 1) * LANE] for c in range(chunks)]
        stripes += [mixed[:, c * LANE:(c + 1) * LANE] for c in range(chunks)]
        per_stripe = half // depth
        for piece in range(pieces):
            stripe, place = piece // per_stripe, piece % per_stripe
            packed_ref[piece, slot * depth:(slot + 1) * depth] = (
                stripes[stripe][place * depth:(place + 1) * depth]
            )
        for c in range(chunks):
            line = diagonal[:, c * LANE:(c + 1) * LANE]
            info = jnp.where(info_row == slot * chunks + c, line, info)
    tail = info_row == hold * chunks
    values = parts_of(square_sum, SQUARE_PARTS)
    for slot in range(hold):
        name = jnp.zeros((1, 1), jnp.float32) + target_ref[0, slot].astype(jnp.float32)
        values += parts_of(name, NAME_PARTS)
    for place, value in enumerate(values):
        info = jnp.where(tail & (info_col == place), value.astype(jnp.float32), info)
    info = info.astype(jnp.bfloat16)
    for piece in range(pieces):
        packed_ref[piece, hold * depth:] = info


def pack(factors, target, pieces):
    hold, width = factors.shape[1], factors.shape[2]
    depth = width * width // 2 // LANE // pieces
    return pl.pallas_call(
        functools.partial(pack_kernel, pieces),
        out_shape=pltpu.VMEM((pieces, hold * depth + INFO_ROWS, LANE), jnp.bfloat16),
        in_specs=[
            pl.BlockSpec(memory_space=pltpu.SMEM),
            pl.BlockSpec(memory_space=pltpu.VMEM),
        ],
        out_specs=pl.BlockSpec(memory_space=pltpu.VMEM),
        name="pack",
    )(target.T, factors)


def select_kernel(hold, name_ref, pieces_ref, chosen_ref, count_ref):
    depth = chosen_ref.shape[2]
    for owner in range(chosen_ref.shape[0]):
        count_ref[owner] = 0
    for block in range(name_ref.shape[0]):
        owner = name_ref[block]
        slot = count_ref[owner]
        count_ref[owner] = slot + 1
        first = (block % hold) * depth
        chosen_ref[owner, slot] = pieces_ref[block // hold, first:first + depth]


def select(names, pieces, hold, owners):
    depth = (pieces.shape[1] - INFO_ROWS) // hold
    return pl.pallas_call(
        functools.partial(select_kernel, hold),
        out_shape=pltpu.VMEM((owners, CAP, depth, LANE), pieces.dtype),
        in_specs=[
            pl.BlockSpec(memory_space=pltpu.SMEM),
            pl.BlockSpec(memory_space=pltpu.VMEM),
        ],
        out_specs=pl.BlockSpec(memory_space=pltpu.VMEM),
        scratch_shapes=[pltpu.SMEM((owners,), jnp.int32)],
        name="select",
    )(names, pltpu.with_memory_space_constraint(pieces, pltpu.VMEM))


def split(value):
    high = value.astype(jnp.bfloat16)
    return high, (value - high.astype(jnp.float32)).astype(jnp.bfloat16)


def dot(left, right):
    return jnp.dot(left, right, preferred_element_type=jnp.float32)


def root_kernel(first, param_ref, packed_ref, diagonal_ref, *rest):
    out_ref, block_ref, high_ref, low_ref = rest[-4:]
    count, width = out_ref.shape[0], out_ref.shape[1]
    half = width // 2
    chunks = half // LANE
    full, top, bottom = slice(0, width), slice(0, half), slice(half, width)
    tiles = ((top, top), (bottom, top), (bottom, bottom))
    row_ids = lax.broadcasted_iota(jnp.int32, (half, half), 0)
    col_ids = lax.broadcasted_iota(jnp.int32, (half, half), 1)
    eye = row_ids == col_ids
    slots = range(count)

    def add_eye(values, scalar):
        there = jnp.where(eye, scalar, 0.0)
        return values[0] + there, values[1], values[2] + there

    def store(slot, place, values):
        for tile, value in zip(tiles, values):
            high, low = split(value)
            high_ref[slot, place, tile[0], tile[1]] = high
            low_ref[slot, place, tile[0], tile[1]] = low
            if tile == (bottom, top):
                high_ref[slot, place, top, bottom] = high.T
                low_ref[slot, place, top, bottom] = low.T

    def dots(left, right):
        def some(rows, cols):
            return dot(
                jnp.concatenate([part(rows, full) for part in left], axis=1),
                jnp.concatenate([part(full, cols) for part in right], axis=0),
            )

        lower = some(bottom, full)
        return some(top, top), lower[:, top], lower[:, bottom]

    def at(ref, *place):
        return lambda rows, cols: ref[place + (rows, cols)]

    def product(slot, left, right):
        high, low = at(high_ref, slot, left), at(low_ref, slot, left)
        return dots(
            [high, low, high],
            [at(high_ref, slot, right), at(high_ref, slot, right), at(low_ref, slot, right)],
        )

    def by_block(slot, left):
        block = at(block_ref, slot)
        return dots([at(high_ref, slot, left), at(low_ref, slot, left)], [block, block])

    def block_tiles(slot):
        return [block_ref[slot, rows, cols].astype(jnp.float32) for rows, cols in tiles]

    inverses = [param_ref[first + slot, 1] for slot in slots]
    for slot in slots:
        lines = packed_ref[:, slot].reshape(-1, LANE)

        def square(place):
            return jnp.concatenate(
                [lines[(place + c) * half:(place + c + 1) * half] for c in range(chunks)], axis=1
            )

        corner = square(0)
        mixed = square(chunks).astype(jnp.float32)
        turned = mixed.T
        upper = jnp.where(row_ids >= col_ids, mixed, turned)
        lower = jnp.where(row_ids < col_ids, mixed, turned)
        lower = jnp.where(eye, diagonal_ref[first + slot:first + slot + 1, :], lower)
        block_ref[slot, top, top] = upper.astype(jnp.bfloat16)
        block_ref[slot, bottom, top] = corner
        block_ref[slot, top, bottom] = corner.T
        block_ref[slot, bottom, bottom] = lower.astype(jnp.bfloat16)
    for slot in slots:
        scaled = [(0.25 * inverses[slot]) * tile for tile in block_tiles(slot)]
        squared = dots([at(block_ref, slot)], [at(block_ref, slot)])
        factor = 0.0625 * inverses[slot] * inverses[slot]
        store(
            slot, 0, add_eye([factor * b - 2.5 * a for a, b in zip(scaled, squared)], 1.5625)
        )
    def tile_sum(slot, place):
        return [
            high_ref[slot, place, rows, cols].astype(jnp.float32)
            + low_ref[slot, place, rows, cols].astype(jnp.float32)
            for rows, cols in tiles
        ]

    for slot in slots:
        turned = by_block(slot, 0)
        squares = tile_sum(slot, 0)
        cubes = [1.25 * a - (0.25 * inverses[slot]) * b for a, b in zip(squares, turned)]
        store(slot, 1, cubes)
        store(slot, 2, [a - 1.25 * b for a, b in zip(cubes, squares)])
    for slot in slots:
        sixth = product(slot, 1, 2)
        scaled = [(0.3125 * inverses[slot]) * tile for tile in block_tiles(slot)]
        store(slot, 0, add_eye([b - a for a, b in zip(scaled, sixth)], 1.5625))
    for slot in slots:
        store(slot, 1, product(slot, 0, 0))
    for slot in slots:
        store(slot, 2, product(slot, 1, 1))
    for slot in slots:
        tail = by_block(slot, 2)
        store(slot, 1, add_eye([-(0.25 * inverses[slot]) * tile for tile in tail], 1.25))
    for slot in slots:
        result = product(slot, 0, 1)
        valid = param_ref[first + slot, 0] > 0.0
        result = [jnp.where(valid, tile * param_ref[first + slot, 2], 0.0) for tile in result]
        for (rows, cols), tile in zip(tiles, result):
            out_ref[slot, rows, cols] = tile
        out_ref[slot, top, bottom] = result[1].T


def root(params, packed, diagonal, first, width, held):
    count = packed.shape[1]
    operands = [params, pltpu.with_memory_space_constraint(packed, pltpu.VMEM), diagonal]
    in_specs = [
        pl.BlockSpec(memory_space=pltpu.SMEM),
        pl.BlockSpec(memory_space=pltpu.VMEM),
        pl.BlockSpec(memory_space=pltpu.VMEM),
    ]
    aliases = {}
    if held is not None:
        operands.append(held)
        in_specs.append(pl.BlockSpec(memory_space=pl.ANY))
        aliases = {3: 0}
    return pl.pallas_call(
        functools.partial(root_kernel, first),
        grid=(1,),
        out_shape=jax.ShapeDtypeStruct((CAP, width, width), jnp.float32),
        in_specs=in_specs,
        out_specs=pl.BlockSpec((count, width, width), lambda i: (first // count, 0, 0)),
        scratch_shapes=[
            pltpu.VMEM((count, width, width), jnp.bfloat16),
            pltpu.VMEM((count, 3, width, width), jnp.bfloat16),
            pltpu.VMEM((count, 3, width, width), jnp.bfloat16),
        ],
        input_output_aliases=aliases,
        cost_estimate=pl.CostEstimate(
            flops=36 * count * width ** 3,
            bytes_accessed=5 * count * width * width,
            transcendentals=0,
        ),
        name="root",
    )(*operands)


def shards(factors, target):
    row_count, col_count = lax.axis_size("row"), lax.axis_size("col")
    devices = row_count * col_count
    hold, width = factors.shape[1], factors.shape[2]
    total = devices * hold
    me = lax.axis_index("row") * col_count + lax.axis_index("col")
    packed = pack(factors, target, devices)
    pieces = lax.all_to_all(packed, AXES, split_axis=0, concat_axis=0, tiled=True)
    lines = hold * width // 2 // LANE
    info = pieces[:, -INFO_ROWS:].astype(jnp.float32)
    tail = info[:, lines]
    named = tail[:, SQUARE_PARTS:SQUARE_PARTS + hold * NAME_PARTS]
    targets = jnp.sum(named.reshape(total, NAME_PARTS), axis=1).astype(jnp.int32)
    squares = jnp.sum(tail[:, :SQUARE_PARTS], axis=1).reshape(row_count, col_count)
    scales = 2.0 * jnp.sqrt(jnp.sum(squares, axis=1) / (col_count * hold * width))
    numbers = jnp.arange(total, dtype=jnp.int32)
    same = targets[:, None] == targets[None, :]
    slots = jnp.sum((same & (numbers[None, :] < numbers[:, None])).astype(jnp.int32), axis=1)
    mine = (slots[None, :] == jnp.arange(CAP)[:, None]) & (targets[None, :] == me)
    valid = jnp.sum(mine.astype(jnp.float32), axis=1)
    per_block = jnp.repeat(scales, col_count * hold)
    scale = jnp.sum(jnp.where(mine, per_block[None, :], 0.0), axis=1)
    scale = jnp.where(valid > 0, scale, 1.0)
    params = jnp.stack([valid, 1.0 / scale, scale ** (-0.25)], axis=1)
    diagonals = info[:, :lines].reshape(total, width // 2)
    diagonal = jnp.sum(jnp.where(mine[:, :, None], diagonals[None], 0.0), axis=1)
    chosen = select(targets, pieces, hold, devices)
    landed = lax.all_to_all(chosen, AXES, split_axis=0, concat_axis=0, tiled=True)
    return root(params, landed, diagonal, 0, width, None)[None]


def solution(mesh):
    return jax.shard_map(
        shards,
        mesh=mesh,
        in_specs=(P(AXES, None, None, None), P(AXES, None)),
        out_specs=P(AXES, None, None, None),
        check_vma=False,
    )
```

time: 76.3 us -> 67.5 us (0.88)
  blocking collectives: 0 us -> 24.8 us
  waiting for transfers between devices: 32 us -> 19.4 us
  starting transfers between devices: 12.5 us -> 2.63 us
  Pallas kernels: 25.8 us -> 17 us
  local copies, waits for them, and re-layouts: 3.34 us -> 0.64 us
    all_to_all x0 -> x1, blocking collectives: none -> 24.8 us  [shards(): lax.all_to_all(packed, AXES, split_axis=0, concat_axis=0, tiled=True)]
    all_to_all x3 -> x1, waiting for transfers between devices: 32 us -> 19.4 us  [shards(): lax.all_to_all(chosen, AXES, split_axis=0, concat_axis=0, tiled=True)]
    all_to_all x3 -> x1, starting transfers between devices: 12.5 us -> 2.63 us  [shards(): lax.all_to_all(chosen, AXES, split_axis=0, concat_axis=0, tiled=True)]
    pallas_call x4 -> x3, Pallas kernels: 25.8 us -> 17 us  [the longest x1 13.4 us: root(): pl.pallas_call(functools.partial(root_kernel, first), grid=(1,), out_shap...]
    unnamed x7 -> x2, local copies, waits for them, and re-layouts: 2.02 us -> 0.01 us
  transfers between devices with their start and end apart: 3 -> 1, of which waited for: 2 -> 1; matrix products, arithmetic and copies ran while one was open for 2% -> 4% of each run, Pallas kernels for 17% -> 0%
where the time goes in v3:
time: 67.5 us; the launch traced here: 67.2 us
  blocking collectives  24.8 us (37%)
  waiting for transfers between devices  19.4 us (29%)
  Pallas kernels  17 us (25%)
  other arithmetic  2.7 us (4%)
  starting transfers between devices  2.63 us (4%)
    all_to_all x1, blocking collectives, shards(): lax.all_to_all(packed, AXES, split_axis=0, concat_axis=0, tiled=True)  24.8 us
    all_to_all x1, waiting for transfers between devices, shards(): lax.all_to_all(chosen, AXES, split_axis=0, concat_axis=0, tiled=True)  19.4 us
    pallas_call x1, Pallas kernels, root(): pl.pallas_call(functools.partial(root_kernel, first), grid=(1,), out_shap...  13.4 us
    all_to_all x1, starting transfers between devices, shards(): lax.all_to_all(chosen, AXES, split_axis=0, concat_axis=0, tiled=True)  2.63 us
    pallas_call x1, Pallas kernels, select(): pl.pallas_call(functools.partial(select_kernel, hold), out_shape=pltpu.VM...  1.96 us
    pallas_call x1, Pallas kernels, pack(): pl.pallas_call(functools.partial(pack_kernel, pieces), out_shape=pltpu.VM...  1.64 us
  transfers between devices with their start and end apart: 1, of which 1 were waited for; matrix products, arithmetic and copies ran while one was open for 4% of the time, Pallas kernels for 0%

profile of v3, /device:TPU:0, one launch (start us, length us, event | category | flops | bytes accessed | tf_op | source)
XLA Modules:
  0.0 67.2 jit_solution(16052740995277819690)
XLA Ops:
  0.0 1.6 %pack.1 = bf16[32,72,128]{2,1,0:T(8,128)(2,1)S(1)} custom-call(s32[1,2]{1,0:T(1,128)} %bitcast.9, bf16[1,2,512,512]{3,2,1,0:T(8,128)(2,1)} %block_ref.1), custom_call_target="tpu_custom_call" | custom-call | tf_op jit(solution)/shard_map/pack/pallas_call | solution.py:73
  1.6 24.8 %all_to_all.10.pieces_ref = bf16[32,72,128]{2,1,0:T(8,128)(2,1)S(1)} all-to-all(bf16[32,72,128]{2,1,0:T(8,128)(2,1)S(1)} %pack.1), channel_id=1, replica_groups=mesh['row'=4,'col'=8] {'row','col'}, dimensions={0} | all-to-all | bytes 1179648 | tf_op jit(solution)/shard_map/all_to_all | solution.py:273
  26.5 0.1 slice.22
  26.5 0.1 reshape.76
  26.6 0.1 reduce_sum.65
  26.7 0.6 convert_element_type.13.name_ref
  27.3 0.0 copy-start
  27.3 2.0 %select.1 = bf16[32,3,32,128]{3,2,1,0:T(8,128)(2,1)} custom-call(s32[64]{0:T(128)} %convert_element_type.13.name_ref, bf16[32,72,128]{2,1,0:T(8,128)(2,1)S(1)} %all_to_all.10.pieces_ref), custom_call_target="tpu_custom_call" | custom-call | tf_op jit(solution)/shard_map/select/pallas_call | solution.py:99
  29.3 2.6 %all-to-all-start.1 = ((bf16[32,3,32,128]{3,2,1,0:T(8,128)(2,1)}), bf16[32,3,32,128]{3,2,1,0:T(8,128)(2,1)S(1)}, u32[]{:S(2)}, u32[]{:S(2)}) async-start(bf16[32,3,32,128]{3,2,1,0:T(8,128)(2,1)} %select.1), calls=%async_computation.1 | async-start | bytes 1572864 | tf_op jit(solution)/shard_map/all_to_all | solution.py:293
  32.0 0.1 slice_reduce_fusion
  32.1 0.1 reshape.77
  32.2 0.1 reduce_sum.69
  32.3 0.1 broadcast_in_dim.52
  32.4 0.1 broadcast_in_dim.53
  32.5 0.0 copy-done
  32.5 0.2 convert_reduce_fusion
  32.7 0.1 convert_reduce_fusion.1
  32.8 0.1 copy.11
  32.9 0.1 copy.10
  33.0 0.7 %pad_maximum_fusion.param_ref = f32[3,3]{1,0:T(4,128)} fusion(f32[3,1]{1,0:T(4,128)S(1)} %get-tuple-element.9, f32[3,1]{1,0:T(4,128)S(1)} %get-tuple-element.8, f32[3,1]{1,0:T(4,128)S(1)} %copy.11), kind=kLoop, calls=%fused_computation.6 | loop fusion | flops 18 | bytes 72 | tf_op jit(solution)/shard_map/stack | solution.py:289
  33.7 0.7 %select_reduce_fusion.diagonal_ref = f32[3,256]{1,0:T(4,128)} fusion(f32[64,256]{1,0:T(8,128)S(1)} %broadcast_in_dim.57, pred[3,64]{1,0:T(4,128)(4,1)S(1)} %get-tuple-element.7), kind=kLoop, calls=%fused_computation | loop fusion | flops 97536 | bytes 68800 | tf_op jit(solution)/shard_map/reduce_sum | solution.py:291
  34.4 19.4 %all-to-all-done.1.packed_ref = bf16[32,3,32,128]{3,2,1,0:T(8,128)(2,1)S(1)} async-done(((bf16[32,3,32,128]{3,2,1,0:T(8,128)(2,1)}), bf16[32,3,32,128]{3,2,1,0:T(8,128)(2,1)S(1)}, u32[]{:S(2)}, u32[]{:S(2)}) %all-to-all-start.1) | async-done | bytes 786464 | tf_op jit(solution)/shard_map/all_to_all | solution.py:293
  53.8 13.4 %root.1 = f32[3,512,512]{2,1,0:T(8,128)} custom-call(f32[3,3]{1,0:T(4,128)} %pad_maximum_fusion.param_ref, bf16[32,3,32,128]{3,2,1,0:T(8,128)(2,1)S(1)} %all-to-all-done.1.packed_ref, f32[3,256]{1,0:T(4,128)} %select_reduce_fusion.diagonal_ref), custom_call_target="tpu_custom_call" | custom-call | flops 14495514624 | bytes 3932160 | tf_op jit(solution)/shard_map/root/pallas_call | solution.py:245
  (7 shorter events, 0.1 us)
Async XLA Ops:
  27.3 5.2 %copy-start = (s32[64]{0:T(128)S(1)}, s32[64]{0:T(128)}, u32[]{:S(2)}) copy-start(s32[64]{0:T(128)} %convert_element_type.13.name_ref) | copy-start | bytes 772
  29.3 24.5 %all-to-all-start.1 = ((bf16[32,3,32,128]{3,2,1,0:T(8,128)(2,1)}), bf16[32,3,32,128]{3,2,1,0:T(8,128)(2,1)S(1)}, u32[]{:S(2)}, u32[]{:S(2)}) async-start(bf16[32,3,32,128]{3,2,1,0:T(8,128)(2,1)} %select.1), calls=%async_computation.1 | async-start | bytes 1572864 | tf_op jit(solution)/shard_map/all_to_all | solution.py:293

commit v4 on v3

--- a/solution.py
+++ b/solution.py
@@ -11,8 +11,8 @@
 INFO_ROWS = 8
 SQUARE_PARTS = 3
 NAME_PARTS = 2
-EARLY = 2
 AXES = ("row", "col")
+RING = ("col", "row")
 
 
 def parts_of(value, count):
@@ -24,8 +24,9 @@
     return parts
 
 
-def pack_kernel(pieces, target_ref, block_ref, packed_ref):
+def pack_kernel(row_count, col_count, target_ref, block_ref, packed_ref):
     hold, width = block_ref.shape[1], block_ref.shape[2]
+    pieces = packed_ref.shape[0]
     half = width // 2
     depth = (packed_ref.shape[1] - INFO_ROWS) // hold
     row_ids = lax.broadcasted_iota(jnp.int32, (half, half), 0)
@@ -58,8 +59,10 @@
     tail = info_row == hold * chunks
     values = parts_of(square_sum, SQUARE_PARTS)
     for slot in range(hold):
-        name = jnp.zeros((1, 1), jnp.float32) + target_ref[0, slot].astype(jnp.float32)
-        values += parts_of(name, NAME_PARTS)
+        owner = target_ref[0, slot]
+        place = lax.rem(owner, col_count) * row_count + lax.div(owner, col_count)
+        place = jnp.zeros((1, 1), jnp.float32) + place.astype(jnp.float32)
+        values += parts_of(place, NAME_PARTS)
     for place, value in enumerate(values):
         info = jnp.where(tail & (info_col == place), value.astype(jnp.float32), info)
     info = info.astype(jnp.bfloat16)
@@ -67,11 +70,12 @@
         packed_ref[piece, hold * depth:] = info
 
 
-def pack(factors, target, pieces):
+def pack(factors, target, row_count, col_count):
     hold, width = factors.shape[1], factors.shape[2]
+    pieces = row_count * col_count
     depth = width * width // 2 // LANE // pieces
     return pl.pallas_call(
-        functools.partial(pack_kernel, pieces),
+        functools.partial(pack_kernel, row_count, col_count),
         out_shape=pltpu.VMEM((pieces, hold * depth + INFO_ROWS, LANE), jnp.bfloat16),
         in_specs=[
             pl.BlockSpec(memory_space=pltpu.SMEM),
@@ -82,31 +86,81 @@
     )(target.T, factors)
 
 
-def select_kernel(hold, name_ref, pieces_ref, chosen_ref, count_ref):
-    depth = chosen_ref.shape[2]
-    for owner in range(chosen_ref.shape[0]):
+def select_kernel(
+    hold, row_count, col_count, width, pieces_ref, chosen_ref, param_ref,
+    name_ref, place_ref, count_ref, table_ref, sem,
+):
+    owners, depth = chosen_ref.shape[0], chosen_ref.shape[2]
+    rows = hold * depth
+    half_lines = width // 2 // LANE
+    info = pieces_ref[:, rows:rows + INFO_ROWS].astype(jnp.float32)
+    tail = info[:, hold * half_lines]
+    names = [tail]
+    for part in range(1, NAME_PARTS):
+        names.append(pltpu.roll(tail, LANE - part, 1))
+    name_ref[...] = sum(names).astype(jnp.int32)
+    copy = pltpu.make_async_copy(name_ref, place_ref, sem)
+    copy.start()
+    for owner in range(owners):
         count_ref[owner] = 0
-    for block in range(name_ref.shape[0]):
-        owner = name_ref[block]
-        slot = count_ref[owner]
-        count_ref[owner] = slot + 1
-        first = (block % hold) * depth
-        chosen_ref[owner, slot] = pieces_ref[block // hold, first:first + depth]
-
-
-def select(names, pieces, hold, owners):
+    copy.wait()
+    for device in range(owners):
+        source = (device % col_count) * row_count + device // col_count
+        for part in range(hold):
+            owner = place_ref[source, SQUARE_PARTS + part * NAME_PARTS]
+            slot = count_ref[owner]
+            count_ref[owner] = slot + 1
+            table_ref[owner, slot] = source * hold + part
+            chosen_ref[owner, slot] = pieces_ref[source, part * depth:(part + 1) * depth]
+    me = lax.axis_index("col") * row_count + lax.axis_index("row")
+    source_ids = lax.broadcasted_iota(jnp.int32, (owners, LANE), 0)
+    lanes = lax.broadcasted_iota(jnp.int32, (owners, LANE), 1)
+    squares = jnp.where(lanes < SQUARE_PARTS, tail, 0.0)
+    for slot in range(CAP):
+        valid = slot < count_ref[me]
+        code = jnp.where(valid, table_ref[me, slot], 0)
+        source, part = lax.div(code, hold), lax.rem(code, hold)
+        same_row = lax.rem(source_ids, row_count) == lax.rem(source, row_count)
+        total = jnp.sum(
+            jnp.sum(jnp.where(same_row, squares, 0.0), axis=0, keepdims=True), axis=1, keepdims=True
+        )
+        scale = 2.0 * jnp.sqrt(total / (col_count * hold * width))
+        inverse = 1.0 / scale
+        gain = lax.rsqrt(jnp.sqrt(scale))
+        here = pieces_ref[source, rows:rows + INFO_ROWS].astype(jnp.float32)
+        diagonal = here[:half_lines]
+        for other in range(1, hold):
+            lines = here[other * half_lines:(other + 1) * half_lines]
+            diagonal = jnp.where(part == other, lines, diagonal)
+        param_ref[slot, :half_lines] = diagonal
+        one = jnp.zeros((1, LANE), jnp.float32)
+        param_ref[slot, half_lines:half_lines + 1] = one + inverse
+        param_ref[slot, half_lines + 1:half_lines + 2] = jnp.where(valid, one + gain, 0.0)
+
+
+def select(pieces, hold, row_count, col_count, width):
+    owners = pieces.shape[0]
     depth = (pieces.shape[1] - INFO_ROWS) // hold
     return pl.pallas_call(
-        functools.partial(select_kernel, hold),
-        out_shape=pltpu.VMEM((owners, CAP, depth, LANE), pieces.dtype),
-        in_specs=[
-            pl.BlockSpec(memory_space=pltpu.SMEM),
-            pl.BlockSpec(memory_space=pltpu.VMEM),
+        functools.partial(select_kernel, hold, row_count, col_count, width),
+        out_shape=(
+            pltpu.VMEM((owners, CAP, depth, LANE), pieces.dtype),
+            pltpu.VMEM((CAP, INFO_ROWS, LANE), jnp.float32),
+        ),
+        in_specs=[pl.BlockSpec(memory_space=pltpu.VMEM)],
+        out_specs=(
+            pl.BlockSpec(memory_space=pltpu.VMEM),
+            pl.BlockSpec(memory_space=pltpu.VMEM),
+        ),
+        scratch_shapes=[
+            pltpu.VMEM((owners, LANE), jnp.int32),
+            pltpu.SMEM((owners, LANE), jnp.int32),
+            pltpu.SMEM((owners,), jnp.int32),
+            pltpu.SMEM((owners, CAP), jnp.int32),
+            pltpu.SemaphoreType.DMA,
         ],
-        out_specs=pl.BlockSpec(memory_space=pltpu.VMEM),
-        scratch_shapes=[pltpu.SMEM((owners,), jnp.int32)],
         name="select",
-    )(names, pltpu.with_memory_space_constraint(pieces, pltpu.VMEM))
+    )(pltpu.with_memory_space_constraint(pieces, pltpu.VMEM))
 
 
 def split(value):
@@ -118,8 +172,7 @@
     return jnp.dot(left, right, preferred_element_type=jnp.float32)
 
 
-def root_kernel(first, param_ref, packed_ref, diagonal_ref, *rest):
-    out_ref, block_ref, high_ref, low_ref = rest[-4:]
+def root_kernel(param_ref, packed_ref, out_ref, made_ref, block_ref, high_ref, low_ref, sem):
     count, width = out_ref.shape[0], out_ref.shape[1]
     half = width // 2
     chunks = half // LANE
@@ -170,7 +223,8 @@
     def block_tiles(slot):
         return [block_ref[slot, rows, cols].astype(jnp.float32) for rows, cols in tiles]
 
-    inverses = [param_ref[first + slot, 1] for slot in slots]
+    inverses = [param_ref[slot, chunks:chunks + 1, :1] for slot in slots]
+    gains = [param_ref[slot, chunks + 1:chunks + 2, :1] for slot in slots]
     for slot in slots:
         lines = packed_ref[:, slot].reshape(-1, LANE)
 
@@ -184,7 +238,8 @@
         turned = mixed.T
         upper = jnp.where(row_ids >= col_ids, mixed, turned)
         lower = jnp.where(row_ids < col_ids, mixed, turned)
-        lower = jnp.where(eye, diagonal_ref[first + slot:first + slot + 1, :], lower)
+        diagonal = jnp.concatenate([param_ref[slot, c:c + 1] for c in range(chunks)], axis=1)
+        lower = jnp.where(eye, diagonal, lower)
         block_ref[slot, top, top] = upper.astype(jnp.bfloat16)
         block_ref[slot, bottom, top] = corner
         block_ref[slot, top, bottom] = corner.T
@@ -220,78 +275,56 @@
     for slot in slots:
         tail = by_block(slot, 2)
         store(slot, 1, add_eye([-(0.25 * inverses[slot]) * tile for tile in tail], 1.25))
-    for slot in slots:
-        result = product(slot, 0, 1)
-        valid = param_ref[first + slot, 0] > 0.0
-        result = [jnp.where(valid, tile * param_ref[first + slot, 2], 0.0) for tile in result]
+    copies = []
+    for slot in slots:
+        valid = gains[slot] > 0.0
+        result = [jnp.where(valid, tile * gains[slot], 0.0) for tile in product(slot, 0, 1)]
         for (rows, cols), tile in zip(tiles, result):
-            out_ref[slot, rows, cols] = tile
-        out_ref[slot, top, bottom] = result[1].T
-
-
-def root(params, packed, diagonal, first, width, held):
+            made_ref[slot, rows, cols] = tile
+        made_ref[slot, top, bottom] = result[1].T
+        copies.append(pltpu.make_async_copy(made_ref.at[slot], out_ref.at[slot], sem.at[slot]))
+        copies[-1].start()
+    for copy in copies:
+        copy.wait()
+
+
+def root(params, packed, width):
     count = packed.shape[1]
-    operands = [params, pltpu.with_memory_space_constraint(packed, pltpu.VMEM), diagonal]
-    in_specs = [
-        pl.BlockSpec(memory_space=pltpu.SMEM),
-        pl.BlockSpec(memory_space=pltpu.VMEM),
-        pl.BlockSpec(memory_space=pltpu.VMEM),
-    ]
-    aliases = {}
-    if held is not None:
-        operands.append(held)
-        in_specs.append(pl.BlockSpec(memory_space=pl.ANY))
-        aliases = {3: 0}
     return pl.pallas_call(
-        functools.partial(root_kernel, first),
-        grid=(1,),
-        out_shape=jax.ShapeDtypeStruct((CAP, width, width), jnp.float32),
-        in_specs=in_specs,
-        out_specs=pl.BlockSpec((count, width, width), lambda i: (first // count, 0, 0)),
+        root_kernel,
+        out_shape=jax.ShapeDtypeStruct((count, width, width), jnp.float32),
+        in_specs=[
+            pl.BlockSpec(memory_space=pltpu.VMEM),
+            pl.BlockSpec(memory_space=pltpu.VMEM),
+        ],
+        out_specs=pl.BlockSpec(memory_space=pl.ANY),
         scratch_shapes=[
+            pltpu.VMEM((count, width, width), jnp.float32),
             pltpu.VMEM((count, width, width), jnp.bfloat16),
             pltpu.VMEM((count, 3, width, width), jnp.bfloat16),
             pltpu.VMEM((count, 3, width, width), jnp.bfloat16),
+            pltpu.SemaphoreType.DMA((count,)),
         ],
-        input_output_aliases=aliases,
         cost_estimate=pl.CostEstimate(
-            flops=36 * count * width ** 3,
+            flops=26 * count * width ** 3,
             bytes_accessed=5 * count * width * width,
             transcendentals=0,
         ),
         name="root",
-    )(*operands)
+    )(
+        pltpu.with_memory_space_constraint(params, pltpu.VMEM),
+        pltpu.with_memory_space_constraint(packed, pltpu.VMEM),
+    )
 
 
 def shards(factors, target):
     row_count, col_count = lax.axis_size("row"), lax.axis_size("col")
-    devices = row_count * col_count
     hold, width = factors.shape[1], factors.shape[2]
-    total = devices * hold
-    me = lax.axis_index("row") * col_count + lax.axis_index("col")
-    packed = pack(factors, target, devices)
-    pieces = lax.all_to_all(packed, AXES, split_axis=0, concat_axis=0, tiled=True)
-    lines = hold * width // 2 // LANE
-    info = pieces[:, -INFO_ROWS:].astype(jnp.float32)
-    tail = info[:, lines]
-    named = tail[:, SQUARE_PARTS:SQUARE_PARTS + hold * NAME_PARTS]
-    targets = jnp.sum(named.reshape(total, NAME_PARTS), axis=1).astype(jnp.int32)
-    squares = jnp.sum(tail[:, :SQUARE_PARTS], axis=1).reshape(row_count, col_count)
-    scales = 2.0 * jnp.sqrt(jnp.sum(squares, axis=1) / (col_count * hold * width))
-    numbers = jnp.arange(total, dtype=jnp.int32)
-    same = targets[:, None] == targets[None, :]
-    slots = jnp.sum((same & (numbers[None, :] < numbers[:, None])).astype(jnp.int32), axis=1)
-    mine = (slots[None, :] == jnp.arange(CAP)[:, None]) & (targets[None, :] == me)
-    valid = jnp.sum(mine.astype(jnp.float32), axis=1)
-    per_block = jnp.repeat(scales, col_count * hold)
-    scale = jnp.sum(jnp.where(mine, per_block[None, :], 0.0), axis=1)
-    scale = jnp.where(valid > 0, scale, 1.0)
-    params = jnp.stack([valid, 1.0 / scale, scale ** (-0.25)], axis=1)
-    diagonals = info[:, :lines].reshape(total, width // 2)
-    diagonal = jnp.sum(jnp.where(mine[:, :, None], diagonals[None], 0.0), axis=1)
-    chosen = select(targets, pieces, hold, devices)
-    landed = lax.all_to_all(chosen, AXES, split_axis=0, concat_axis=0, tiled=True)
-    return root(params, landed, diagonal, 0, width, None)[None]
+    packed = pack(factors, target, row_count, col_count)
+    pieces = lax.all_to_all(packed, RING, split_axis=0, concat_axis=0, tiled=True)
+    chosen, params = select(pieces, hold, row_count, col_count, width)
+    landed = lax.all_to_all(chosen, RING, split_axis=0, concat_axis=0, tiled=True)
+    return root(params, landed, width)[None]
 
 
 def solution(mesh):

time: 67.5 us -> 62.9 us (0.932)
  blocking collectives: 24.8 us -> 47.5 us
  waiting for transfers between devices: 19.4 us -> 0 us
  other arithmetic: 2.7 us -> 0 us
  starting transfers between devices: 2.63 us -> 0 us
  Pallas kernels: 17 us -> 15.1 us
    all_to_all x1 -> x2, blocking collectives: 24.8 us -> 47.5 us  [the longest x1 23.9 us: shards(): lax.all_to_all(packed, RING, split_axis=0, concat_axis=0, tiled=True)]
    all_to_all x1 -> x0, waiting for transfers between devices: 19.4 us -> none  [shards(): lax.all_to_all(chosen, AXES, split_axis=0, concat_axis=0, tiled=True)]
    all_to_all x1 -> x0, starting transfers between devices: 2.63 us -> none  [shards(): lax.all_to_all(chosen, AXES, split_axis=0, concat_axis=0, tiled=True)]
    pallas_call x3, Pallas kernels: 17 us -> 15.1 us  [the longest x1 12.2 us: root(): pl.pallas_call(root_kernel, out_shape=jax.ShapeDtypeStruct((count, width,...]
    reduce_sum x6 -> x0, other arithmetic: 1.37 us -> none  [the longest x1 0.7 us: shards(): jnp.sum(jnp.where(mine[:, :, None], diagonals[None], 0.0), axis=1)]
  transfers between devices with their start and end apart: 1 -> 0, of which waited for: 1 -> 0; matrix products, arithmetic and copies ran while one was open for 4% -> 0% of each run, Pallas kernels for 0% -> 0%
where the time goes in v4:
time: 62.9 us; the launch traced here: 62.7 us
  blocking collectives  47.5 us (76%)
  Pallas kernels  15.1 us (24%)
    all_to_all x1, blocking collectives, shards(): lax.all_to_all(packed, RING, split_axis=0, concat_axis=0, tiled=True)  23.9 us
    all_to_all x1, blocking collectives, shards(): lax.all_to_all(chosen, RING, split_axis=0, concat_axis=0, tiled=True)  23.6 us
    pallas_call x1, Pallas kernels, root(): pl.pallas_call(root_kernel, out_shape=jax.ShapeDtypeStruct((count, width,...  12.2 us
    pallas_call x1, Pallas kernels, pack(): pl.pallas_call(functools.partial(pack_kernel, row_count, col_count), out_...  1.64 us
    pallas_call x1, Pallas kernels, select(): pl.pallas_call(functools.partial(select_kernel, hold, row_count, col_coun...  1.35 us

profile of v4, /device:TPU:0, one launch (start us, length us, event | category | flops | bytes accessed | tf_op | source)
XLA Modules:
  0.0 62.7 jit_solution(12648977670858426437)
XLA Ops:
  0.0 1.6 %pack.1 = bf16[32,72,128]{2,1,0:T(8,128)(2,1)S(1)} custom-call(s32[1,2]{1,0:T(1,128)} %bitcast.2, bf16[1,2,512,512]{3,2,1,0:T(8,128)(2,1)} %block_ref.1), custom_call_target="tpu_custom_call" | custom-call | tf_op jit(solution)/shard_map/pack/pallas_call | solution.py:77
  1.6 23.9 %all_to_all.10.pieces_ref = bf16[32,72,128]{2,1,0:T(8,128)(2,1)S(1)} all-to-all(bf16[32,72,128]{2,1,0:T(8,128)(2,1)S(1)} %pack.1), channel_id=1, replica_groups=mesh['row'=4,'col'=8] {'col','row'}, dimensions={0} | all-to-all | bytes 1179648 | tf_op jit(solution)/shard_map/all_to_all | solution.py:324
  25.6 1.3 %select.1 = (bf16[32,3,32,128]{3,2,1,0:T(8,128)(2,1)S(1)}, f32[3,8,128]{2,1,0:T(8,128)S(1)}) custom-call(bf16[32,72,128]{2,1,0:T(8,128)(2,1)S(1)} %all_to_all.10.pieces_ref), custom_call_target="tpu_custom_call" | custom-call | tf_op jit(solution)/shard_map/select/pallas_call | solution.py:144
  26.9 23.6 %all_to_all.11.packed_ref = bf16[32,3,32,128]{3,2,1,0:T(8,128)(2,1)S(1)} all-to-all(bf16[32,3,32,128]{3,2,1,0:T(8,128)(2,1)S(1)} %get-tuple-element.8), channel_id=1, replica_groups=mesh['row'=4,'col'=8] {'col','row'}, dimensions={0} | all-to-all | bytes 1572864 | tf_op jit(solution)/shard_map/all_to_all | solution.py:326
  50.5 12.2 %root.1 = f32[3,512,512]{2,1,0:T(8,128)} custom-call(f32[3,8,128]{2,1,0:T(8,128)S(1)} %get-tuple-element.7.param_ref, bf16[32,3,32,128]{3,2,1,0:T(8,128)(2,1)S(1)} %all_to_all.11.packed_ref), custom_call_target="tpu_custom_call" | custom-call | flops 10468982784 | bytes 3932160 | tf_op jit(solution)/shard_map/root/pallas_call | solution.py:293

commit v5 on v4

--- a/solution.py
+++ b/solution.py
@@ -11,6 +11,7 @@
 INFO_ROWS = 8
 SQUARE_PARTS = 3
 NAME_PARTS = 2
+LINEAR = -0.625
 AXES = ("row", "col")
 RING = ("col", "row")
 
@@ -203,8 +204,8 @@
                 jnp.concatenate([part(full, cols) for part in right], axis=0),
             )
 
-        lower = some(bottom, full)
-        return some(top, top), lower[:, top], lower[:, bottom]
+        left_half = some(full, top)
+        return left_half[top], left_half[bottom], some(bottom, bottom)
 
     def at(ref, *place):
         return lambda rows, cols: ref[place + (rows, cols)]
@@ -216,6 +217,16 @@
             [at(high_ref, slot, right), at(high_ref, slot, right), at(low_ref, slot, right)],
         )
 
+    def square_of(slot, place):
+        high, low = at(high_ref, slot, place), at(low_ref, slot, place)
+        main = dots([high], [high])
+        cross = dot(high(full, full), low(full, full)).astype(jnp.bfloat16)
+        flipped = [cross[top, top].T, cross[top, bottom].T, cross[bottom, bottom].T]
+        return [
+            value + (cross[tile[0], tile[1]].astype(jnp.float32) + other.astype(jnp.float32))
+            for value, tile, other in zip(main, tiles, flipped)
+        ]
+
     def by_block(slot, left):
         block = at(block_ref, slot)
         return dots([at(high_ref, slot, left), at(low_ref, slot, left)], [block, block])
@@ -234,8 +245,9 @@
             )
 
         corner = square(0)
-        mixed = square(chunks).astype(jnp.float32)
-        turned = mixed.T
+        mixed = square(chunks)
+        turned = mixed.T.astype(jnp.float32)
+        mixed = mixed.astype(jnp.float32)
         upper = jnp.where(row_ids >= col_ids, mixed, turned)
         lower = jnp.where(row_ids < col_ids, mixed, turned)
         diagonal = jnp.concatenate([param_ref[slot, c:c + 1] for c in range(chunks)], axis=1)
@@ -244,7 +256,6 @@
         block_ref[slot, bottom, top] = corner
         block_ref[slot, top, bottom] = corner.T
         block_ref[slot, bottom, bottom] = lower.astype(jnp.bfloat16)
-    for slot in slots:
         scaled = [(0.25 * inverses[slot]) * tile for tile in block_tiles(slot)]
         squared = dots([at(block_ref, slot)], [at(block_ref, slot)])
         factor = 0.0625 * inverses[slot] * inverses[slot]
@@ -258,20 +269,28 @@
             for rows, cols in tiles
         ]
 
+    second = -0.5 * LINEAR * LINEAR
+    third = -LINEAR * second
+    pairs = []
     for slot in slots:
         turned = by_block(slot, 0)
         squares = tile_sum(slot, 0)
-        cubes = [1.25 * a - (0.25 * inverses[slot]) * b for a, b in zip(squares, turned)]
-        store(slot, 1, cubes)
-        store(slot, 2, [a - 1.25 * b for a, b in zip(cubes, squares)])
-    for slot in slots:
-        sixth = product(slot, 1, 2)
-        scaled = [(0.3125 * inverses[slot]) * tile for tile in block_tiles(slot)]
-        store(slot, 0, add_eye([b - a for a, b in zip(scaled, sixth)], 1.5625))
-    for slot in slots:
-        store(slot, 1, product(slot, 0, 0))
-    for slot in slots:
-        store(slot, 2, product(slot, 1, 1))
+        scaled = [(0.25 * inverses[slot]) * tile for tile in block_tiles(slot)]
+        near = [
+            (1.25 + LINEAR) * b - (0.25 * inverses[slot]) * c - second * a
+            for a, b, c in zip(scaled, squares, turned)
+        ]
+        store(slot, 1, add_eye(near, 1.25 * second + third))
+        from_square = second * second + 2.0 * LINEAR * third
+        from_step = 2.0 * second * third - 1.25
+        rest = [from_step * a - from_square * b for a, b in zip(scaled, squares)]
+        pairs.append(add_eye(rest, -1.25 * from_step - third * third))
+    for slot in slots:
+        store(slot, 0, [a + b for a, b in zip(square_of(slot, 1), pairs[slot])])
+    for slot in slots:
+        store(slot, 1, square_of(slot, 0))
+    for slot in slots:
+        store(slot, 2, square_of(slot, 1))
     for slot in slots:
         tail = by_block(slot, 2)
         store(slot, 1, add_eye([-(0.25 * inverses[slot]) * tile for tile in tail], 1.25))
@@ -279,11 +298,20 @@
     for slot in slots:
         valid = gains[slot] > 0.0
         result = [jnp.where(valid, tile * gains[slot], 0.0) for tile in product(slot, 0, 1)]
-        for (rows, cols), tile in zip(tiles, result):
-            made_ref[slot, rows, cols] = tile
-        made_ref[slot, top, bottom] = result[1].T
-        copies.append(pltpu.make_async_copy(made_ref.at[slot], out_ref.at[slot], sem.at[slot]))
-        copies[-1].start()
+        for place, rows in enumerate((bottom, top)):
+            if rows == bottom:
+                made_ref[slot, bottom, top] = result[1]
+                made_ref[slot, bottom, bottom] = result[2]
+            else:
+                made_ref[slot, top, top] = result[0]
+                made_ref[slot, top, bottom] = result[1].T
+            span = pl.ds(rows.start, half)
+            copies.append(
+                pltpu.make_async_copy(
+                    made_ref.at[slot, span], out_ref.at[slot, span], sem.at[slot, place]
+                )
+            )
+            copies[-1].start()
     for copy in copies:
         copy.wait()
 
@@ -303,7 +331,7 @@
             pltpu.VMEM((count, width, width), jnp.bfloat16),
             pltpu.VMEM((count, 3, width, width), jnp.bfloat16),
             pltpu.VMEM((count, 3, width, width), jnp.bfloat16),
-            pltpu.SemaphoreType.DMA((count,)),
+            pltpu.SemaphoreType.DMA((count, 2)),
         ],
         cost_estimate=pl.CostEstimate(
             flops=26 * count * width ** 3,

time: 62.9 us -> 61.9 us (0.984)
  Pallas kernels: 15.1 us -> 14.2 us
    pallas_call x1, Pallas kernels: 12.2 us -> 11.2 us  [root(): pl.pallas_call(root_kernel, out_shape=jax.ShapeDtypeStruct((count, width,...]
where the time goes in v5:
time: 61.9 us; the launch traced here: 61.7 us
  blocking collectives  47.5 us (77%)
  Pallas kernels  14.2 us (23%)
    all_to_all x1, blocking collectives, shards(): lax.all_to_all(packed, RING, split_axis=0, concat_axis=0, tiled=True)  23.9 us
    all_to_all x1, blocking collectives, shards(): lax.all_to_all(chosen, RING, split_axis=0, concat_axis=0, tiled=True)  23.6 us
    pallas_call x1, Pallas kernels, root(): pl.pallas_call(root_kernel, out_shape=jax.ShapeDtypeStruct((count, width,...  11.2 us
    pallas_call x1, Pallas kernels, pack(): pl.pallas_call(functools.partial(pack_kernel, row_count, col_count), out_...  1.64 us
    pallas_call x1, Pallas kernels, select(): pl.pallas_call(functools.partial(select_kernel, hold, row_count, col_coun...  1.35 us

profile of v5, /device:TPU:0, one launch (start us, length us, event | category | flops | bytes accessed | tf_op | source)
XLA Modules:
  0.0 61.7 jit_solution(11881887947460853166)
XLA Ops:
  0.0 1.6 %pack.1 = bf16[32,72,128]{2,1,0:T(8,128)(2,1)S(1)} custom-call(s32[1,2]{1,0:T(1,128)} %bitcast.2, bf16[1,2,512,512]{3,2,1,0:T(8,128)(2,1)} %block_ref.1), custom_call_target="tpu_custom_call" | custom-call | tf_op jit(solution)/shard_map/pack/pallas_call | solution.py:78
  1.6 23.9 %all_to_all.10.pieces_ref = bf16[32,72,128]{2,1,0:T(8,128)(2,1)S(1)} all-to-all(bf16[32,72,128]{2,1,0:T(8,128)(2,1)S(1)} %pack.1), channel_id=1, replica_groups=mesh['row'=4,'col'=8] {'col','row'}, dimensions={0} | all-to-all | bytes 1179648 | tf_op jit(solution)/shard_map/all_to_all | solution.py:352
  25.6 1.3 %select.1 = (bf16[32,3,32,128]{3,2,1,0:T(8,128)(2,1)S(1)}, f32[3,8,128]{2,1,0:T(8,128)S(1)}) custom-call(bf16[32,72,128]{2,1,0:T(8,128)(2,1)S(1)} %all_to_all.10.pieces_ref), custom_call_target="tpu_custom_call" | custom-call | tf_op jit(solution)/shard_map/select/pallas_call | solution.py:145
  26.9 23.6 %all_to_all.11.packed_ref = bf16[32,3,32,128]{3,2,1,0:T(8,128)(2,1)S(1)} all-to-all(bf16[32,3,32,128]{3,2,1,0:T(8,128)(2,1)S(1)} %get-tuple-element.8), channel_id=1, replica_groups=mesh['row'=4,'col'=8] {'col','row'}, dimensions={0} | all-to-all | bytes 1572864 | tf_op jit(solution)/shard_map/all_to_all | solution.py:354
  50.5 11.2 %root.1 = f32[3,512,512]{2,1,0:T(8,128)} custom-call(f32[3,8,128]{2,1,0:T(8,128)S(1)} %get-tuple-element.7.param_ref, bf16[32,3,32,128]{3,2,1,0:T(8,128)(2,1)S(1)} %all_to_all.11.packed_ref), custom_call_target="tpu_custom_call" | custom-call | flops 10468982784 | bytes 3932160 | tf_op jit(solution)/shard_map/root/pallas_call | solution.py:321

commit v6 on v5

--- a/solution.py
+++ b/solution.py
@@ -89,7 +89,7 @@
 
 def select_kernel(
     hold, row_count, col_count, width, pieces_ref, chosen_ref, param_ref,
-    name_ref, place_ref, count_ref, table_ref, sem,
+    count_ref, table_ref,
 ):
     owners, depth = chosen_ref.shape[0], chosen_ref.shape[2]
     rows = hold * depth
@@ -99,16 +99,13 @@
     names = [tail]
     for part in range(1, NAME_PARTS):
         names.append(pltpu.roll(tail, LANE - part, 1))
-    name_ref[...] = sum(names).astype(jnp.int32)
-    copy = pltpu.make_async_copy(name_ref, place_ref, sem)
-    copy.start()
+    places = sum(names).astype(jnp.int32)
     for owner in range(owners):
         count_ref[owner] = 0
-    copy.wait()
     for device in range(owners):
         source = (device % col_count) * row_count + device // col_count
         for part in range(hold):
-            owner = place_ref[source, SQUARE_PARTS + part * NAME_PARTS]
+            owner = places[source, SQUARE_PARTS + part * NAME_PARTS]
             slot = count_ref[owner]
             count_ref[owner] = slot + 1
             table_ref[owner, slot] = source * hold + part
@@ -154,11 +151,8 @@
             pl.BlockSpec(memory_space=pltpu.VMEM),
         ),
         scratch_shapes=[
-            pltpu.VMEM((owners, LANE), jnp.int32),
-            pltpu.SMEM((owners, LANE), jnp.int32),
             pltpu.SMEM((owners,), jnp.int32),
             pltpu.SMEM((owners, CAP), jnp.int32),
-            pltpu.SemaphoreType.DMA,
         ],
         name="select",
     )(pltpu.with_memory_space_constraint(pieces, pltpu.VMEM))

time: 61.9 us -> 61.3 us (level)
  no operation moved by 1% of the time
where the time goes in v6:
time: 61.3 us; the launch traced here: 61.1 us
  blocking collectives  47.5 us (77%)
  Pallas kernels  13.6 us (22%)
    all_to_all x1, blocking collectives, shards(): lax.all_to_all(packed, RING, split_axis=0, concat_axis=0, tiled=True)  23.9 us
    all_to_all x1, blocking collectives, shards(): lax.all_to_all(chosen, RING, split_axis=0, concat_axis=0, tiled=True)  23.6 us
    pallas_call x1, Pallas kernels, root(): pl.pallas_call(root_kernel, out_shape=jax.ShapeDtypeStruct((count, width,...  11.2 us
    pallas_call x1, Pallas kernels, pack(): pl.pallas_call(functools.partial(pack_kernel, row_count, col_count), out_...  1.64 us

profile of v6, /device:TPU:0, one launch (start us, length us, event | category | flops | bytes accessed | tf_op | source)
XLA Modules:
  0.0 61.1 jit_solution(18219002568395902541)
XLA Ops:
  0.0 1.6 %pack.1 = bf16[32,72,128]{2,1,0:T(8,128)(2,1)S(1)} custom-call(s32[1,2]{1,0:T(1,128)} %bitcast.2, bf16[1,2,512,512]{3,2,1,0:T(8,128)(2,1)} %block_ref.1), custom_call_target="tpu_custom_call" | custom-call | tf_op jit(solution)/shard_map/pack/pallas_call | solution.py:78
  1.6 23.9 %all_to_all.10.pieces_ref = bf16[32,72,128]{2,1,0:T(8,128)(2,1)S(1)} all-to-all(bf16[32,72,128]{2,1,0:T(8,128)(2,1)S(1)} %pack.1), channel_id=1, replica_groups=mesh['row'=4,'col'=8] {'col','row'}, dimensions={0} | all-to-all | bytes 1179648 | tf_op jit(solution)/shard_map/all_to_all | solution.py:346
  25.6 0.7 %select.1 = (bf16[32,3,32,128]{3,2,1,0:T(8,128)(2,1)S(1)}, f32[3,8,128]{2,1,0:T(8,128)S(1)}) custom-call(bf16[32,72,128]{2,1,0:T(8,128)(2,1)S(1)} %all_to_all.10.pieces_ref), custom_call_target="tpu_custom_call" | custom-call | tf_op jit(solution)/shard_map/select/pallas_call | solution.py:142
  26.3 23.6 %all_to_all.11.packed_ref = bf16[32,3,32,128]{3,2,1,0:T(8,128)(2,1)S(1)} all-to-all(bf16[32,3,32,128]{3,2,1,0:T(8,128)(2,1)S(1)} %get-tuple-element.8), channel_id=1, replica_groups=mesh['row'=4,'col'=8] {'col','row'}, dimensions={0} | all-to-all | bytes 1572864 | tf_op jit(solution)/shard_map/all_to_all | solution.py:348
  49.9 11.2 %root.1 = f32[3,512,512]{2,1,0:T(8,128)} custom-call(f32[3,8,128]{2,1,0:T(8,128)S(1)} %get-tuple-element.7.param_ref, bf16[32,3,32,128]{3,2,1,0:T(8,128)(2,1)S(1)} %all_to_all.11.packed_ref), custom_call_target="tpu_custom_call" | custom-call | flops 10468982784 | bytes 3932160 | tf_op jit(solution)/shard_map/root/pallas_call | solution.py:315

commit v7 on v6

--- a/solution.py
+++ b/solution.py
@@ -25,8 +25,9 @@
     return parts
 
 
-def pack_kernel(row_count, col_count, target_ref, block_ref, packed_ref):
-    hold, width = block_ref.shape[1], block_ref.shape[2]
+def pack_kernel(row_count, col_count, target_ref, *refs):
+    packed_ref, block_refs = refs[-1], refs[:-1]
+    hold, width = len(block_refs) // 2, block_refs[0].shape[2]
     pieces = packed_ref.shape[0]
     half = width // 2
     depth = (packed_ref.shape[1] - INFO_ROWS) // hold
@@ -38,9 +39,10 @@
     square_sum = jnp.zeros((1, 1), jnp.float32)
     chunks = half // LANE
     for slot in range(hold):
-        upper = block_ref[0, slot, :half, :half].astype(jnp.float32)
-        corner = block_ref[0, slot, half:, :half]
-        lower = block_ref[0, slot, half:, half:].astype(jnp.float32)
+        left_ref, lower_ref = block_refs[2 * slot:2 * slot + 2]
+        upper = left_ref[0, 0, :half].astype(jnp.float32)
+        corner = left_ref[0, 0, half:]
+        lower = lower_ref[0, 0].astype(jnp.float32)
         wide = corner.astype(jnp.float32)
         folded = upper * upper + lower * lower + 2.0 * (wide * wide)
         square_sum = square_sum + jnp.sum(jnp.sum(folded, axis=0, keepdims=True), axis=1, keepdims=True)
@@ -75,16 +77,19 @@
     hold, width = factors.shape[1], factors.shape[2]
     pieces = row_count * col_count
     depth = width * width // 2 // LANE // pieces
+    half = width // 2
+    in_specs = [pl.BlockSpec(memory_space=pltpu.SMEM)]
+    for slot in range(hold):
+        in_specs.append(pl.BlockSpec((1, 1, width, half), lambda i, slot=slot: (0, slot, 0, 0)))
+        in_specs.append(pl.BlockSpec((1, 1, half, half), lambda i, slot=slot: (0, slot, 1, 1)))
     return pl.pallas_call(
         functools.partial(pack_kernel, row_count, col_count),
         out_shape=pltpu.VMEM((pieces, hold * depth + INFO_ROWS, LANE), jnp.bfloat16),
-        in_specs=[
-            pl.BlockSpec(memory_space=pltpu.SMEM),
-            pl.BlockSpec(memory_space=pltpu.VMEM),
-        ],
+        grid=(1,),
+        in_specs=in_specs,
         out_specs=pl.BlockSpec(memory_space=pltpu.VMEM),
         name="pack",
-    )(target.T, factors)
+    )(target.T, *([factors] * (2 * hold)))
 
 
 def select_kernel(

time: 61.3 us -> 61.2 us (level)
  no operation moved by 1% of the time
where the time goes in v7:
time: 61.2 us; the launch traced here: 61 us
  blocking collectives  47.5 us (78%)
  Pallas kernels  13.5 us (22%)
    all_to_all x1, blocking collectives, shards(): lax.all_to_all(packed, RING, split_axis=0, concat_axis=0, tiled=True)  23.9 us
    all_to_all x1, blocking collectives, shards(): lax.all_to_all(chosen, RING, split_axis=0, concat_axis=0, tiled=True)  23.6 us
    pallas_call x1, Pallas kernels, root(): pl.pallas_call(root_kernel, out_shape=jax.ShapeDtypeStruct((count, width,...  11.2 us
    pallas_call x1, Pallas kernels, pack(): pl.pallas_call(functools.partial(pack_kernel, row_count, col_count), out_...  1.55 us

profile of v7, /device:TPU:0, one launch (start us, length us, event | category | flops | bytes accessed | tf_op | source)
XLA Modules:
  0.0 61.0 jit_solution(16705704121408529141)
XLA Ops:
  0.0 1.5 %pack.1 = bf16[32,72,128]{2,1,0:T(8,128)(2,1)S(1)} custom-call(s32[1,2]{1,0:T(1,128)} %bitcast.2, bf16[1,2,512,512]{3,2,1,0:T(8,128)(2,1)} %refs_3_.1, bf16[1,2,512,512]{3,2,1,0:T(8,128)(2,1)} %refs_3_.1, bf16[1,2,512,512]{3,2,1,0:T(8,128)(2,1)} %refs_3_.1, bf16[1,2,512,512]{3,2,1,0:T(8,128)(2,1)} %refs_3_.1), custom_call_target="tpu_custom_call" | custom-call | tf_op jit(solution)/shard_map/pack/pallas_call | solution.py:85
  1.6 23.9 %all_to_all.10.pieces_ref = bf16[32,72,128]{2,1,0:T(8,128)(2,1)S(1)} all-to-all(bf16[32,72,128]{2,1,0:T(8,128)(2,1)S(1)} %pack.1), channel_id=1, replica_groups=mesh['row'=4,'col'=8] {'col','row'}, dimensions={0} | all-to-all | bytes 1179648 | tf_op jit(solution)/shard_map/all_to_all | solution.py:351
  25.5 0.7 %select.1 = (bf16[32,3,32,128]{3,2,1,0:T(8,128)(2,1)S(1)}, f32[3,8,128]{2,1,0:T(8,128)S(1)}) custom-call(bf16[32,72,128]{2,1,0:T(8,128)(2,1)S(1)} %all_to_all.10.pieces_ref), custom_call_target="tpu_custom_call" | custom-call | tf_op jit(solution)/shard_map/select/pallas_call | solution.py:147
  26.2 23.6 %all_to_all.11.packed_ref = bf16[32,3,32,128]{3,2,1,0:T(8,128)(2,1)S(1)} all-to-all(bf16[32,3,32,128]{3,2,1,0:T(8,128)(2,1)S(1)} %get-tuple-element.8), channel_id=1, replica_groups=mesh['row'=4,'col'=8] {'col','row'}, dimensions={0} | all-to-all | bytes 1572864 | tf_op jit(solution)/shard_map/all_to_all | solution.py:353
  49.8 11.2 %root.1 = f32[3,512,512]{2,1,0:T(8,128)} custom-call(f32[3,8,128]{2,1,0:T(8,128)S(1)} %get-tuple-element.7.param_ref, bf16[32,3,32,128]{3,2,1,0:T(8,128)(2,1)S(1)} %all_to_all.11.packed_ref), custom_call_target="tpu_custom_call" | custom-call | flops 10468982784 | bytes 3932160 | tf_op jit(solution)/shard_map/root/pallas_call | solution.py:320
